TPU v7x, 32 devices: a whole 2x2x4 slice. The times are simulated.
32 devices in a mesh: rep: 4 (over y, x), tp: 8 (over z, core).
Axes of the slice: x: 2, y: 2, z: 4, core: 2. Of those that a mesh axis runs over, the one named last changes fastest.
Arguments:
- residual: bfloat16 [4, 1024, 4096], P('rep', 'tp'), may hold values from -6 to 6
- gate_pre: bfloat16 [4, 1024, 7168], P('rep', None, 'tp'), may hold values from -6 to 6
- up_pre: bfloat16 [4, 1024, 7168], P('rep', None, 'tp'), may hold values from -6 to 6
- down_weight: bfloat16 [7168, 4096], P('tp'), may hold values from -0.0625 to 0.0625
- d_out: bfloat16 [4, 1024, 4096], P('rep', 'tp'), may hold values from -1.5 to 1.5
- comp_index: int32 [4, 112, 2048], P('rep', 'tp'), may hold values from 0 to 4095
- comp_value: bfloat16 [4, 112, 2048], P('rep', 'tp'), may hold values from -48 to 48
Outputs:
- output: bfloat16 [4, 1024, 4096], P('rep', 'tp')
- gate_preact_gradient: bfloat16 [4, 1024, 7168], P('rep', None, 'tp')
- up_grad: bfloat16 [4, 1024, 7168], P('rep', None, 'tp')
- weight_grad: bfloat16 [4, 7168, 4096], P('rep', 'tp')
- update: bfloat16 [7168, 4096], P('tp')
- updated_down_weight: bfloat16 [7168, 4096], P('tp')
Inputs may be any that keep to these rules, and one draw needn't show every extreme that they name: `comp_index`: positions of one list may repeat.
All inputs are finite; a program needn't handle non-finite values.
Results may differ from a plain program's by a relative error of at most 0.011.
Values may be sent and summed in bfloat16 or wider, within the bound.
A program may use at most 320 MiB of HBM per device.

v0:
```python
import functools

import jax
import jax.numpy as jnp
import numpy as np
from jax import lax
from jax.experimental import pallas as pl
from jax.experimental.pallas import tpu as pltpu
from jax.sharding import PartitionSpec as P

SPAN = 64
TOPK = 32


learn_rate = 0.02


LANES = 128


def cosine_table(length):
    freq = np.arange(length, dtype=np.float64)[:, None]
    place = np.arange(length, dtype=np.float64)[None, :]
    scales = np.where(freq == 0, np.sqrt(1.0 / length), np.sqrt(2.0 / length))
    return scales * np.cos(np.pi * (2.0 * place + 1.0) * freq / (2.0 * length))


def decode_kernel(count, *refs):
    index_refs, value_refs = refs[:count], refs[count:2 * count]
    weight_ref, right_ref, left_ref, update_ref, weight_out_ref, mixed_ref = refs[2 * count:]
    groups = index_refs[0].shape[1] // LANES
    per_group = LANES // TOPK
    width = per_group * SPAN
    depth = count * LANES
    lane = lax.broadcasted_iota(jnp.int32, (1, depth), 1)
    shift = ((lane // TOPK) % per_group) * SPAN
    row_place = lax.broadcasted_iota(jnp.int32, (SPAN, depth), 0).astype(jnp.float32).astype(jnp.bfloat16)
    col_place = lax.broadcasted_iota(jnp.int32, (width, depth), 0).astype(jnp.float32).astype(jnp.bfloat16)

    def gather(group, carry):
        at = pl.ds(pl.multiple_of(group * LANES, LANES), LANES)
        words = jnp.concatenate([ref[:, at] for ref in index_refs], axis=1)
        values = jnp.concatenate([ref[:, at] for ref in value_refs], axis=1).astype(jnp.bfloat16)
        rows = (words >> (SPAN.bit_length() - 1)).astype(jnp.float32).astype(jnp.bfloat16)
        cols = ((words & (SPAN - 1)) + shift).astype(jnp.float32).astype(jnp.bfloat16)
        row_hot = jnp.where(rows == row_place, values, jnp.bfloat16(0))
        col_hot = jnp.where(cols == col_place, jnp.bfloat16(1), jnp.bfloat16(0))
        spectral = lax.dot_general(
            row_hot, col_hot, (((1,), (1,)), ((), ())), preferred_element_type=jnp.float32
        )
        mixed_ref[pl.ds(pl.multiple_of(group * SPAN, SPAN), SPAN), :] = spectral.astype(jnp.bfloat16)
        return carry

    lax.fori_loop(0, groups, gather, 0, unroll=UNROLL)
    halfway = jnp.dot(
        mixed_ref[...], right_ref[...], preferred_element_type=jnp.float32
    ).astype(jnp.bfloat16)
    for group in range(groups):
        block = jnp.dot(
            left_ref[...], halfway[group * SPAN:(group + 1) * SPAN], preferred_element_type=jnp.float32
        )
        change = (block * (1.0 / count)).astype(jnp.bfloat16)
        at = slice(group * width, (group + 1) * width)
        update_ref[:, at] = change
        weight_out_ref[:, at] = (
            weight_ref[:, at].astype(jnp.float32) - learn_rate * change.astype(jnp.float32)
        ).astype(jnp.bfloat16)


UNROLL = 4


def decode(indices, values, down_weight):
    count = len(indices)
    span_rows, _, listed = indices[0].shape
    units, model = down_weight.shape
    basis = cosine_table(SPAN)
    per_group = LANES // TOPK
    width = per_group * SPAN
    right = jnp.asarray(np.kron(np.eye(per_group), basis), jnp.bfloat16)
    left = jnp.asarray(basis.T, jnp.bfloat16)
    strip = pl.BlockSpec((SPAN, model), lambda a: (a, 0))
    whole = lambda shape: pl.BlockSpec(shape, lambda a: (0, 0))
    return pl.pallas_call(
        functools.partial(decode_kernel, count),
        grid=(span_rows,),
        out_shape=[jax.ShapeDtypeStruct((units, model), jnp.bfloat16)] * 2,
        in_specs=[pl.BlockSpec((None, 1, listed), lambda a: (a, 0, 0))] * (2 * count)
        + [strip, whole((width, width)), whole((SPAN, SPAN))],
        out_specs=[strip, strip],
        scratch_shapes=[pltpu.VMEM((listed // LANES * SPAN, width), jnp.bfloat16)],
        compiler_params=pltpu.CompilerParams(
            dimension_semantics=("arbitrary",), vmem_limit_bytes=24 * 2**20
        ),
        cost_estimate=pl.CostEstimate(
            flops=20 * 10**9, bytes_accessed=units * model * 6, transcendentals=0
        ),
        name="decode",
    )(*indices, *values, down_weight, right, left)


def shards(residual, gate_pre, up_pre, down_weight, d_out, comp_index, comp_value):
    residual_r = residual[0]
    gate_r = gate_pre[0]
    up_r = up_pre[0]
    grads_r = d_out[0]
    replicas = lax.axis_size("rep")

    def from_replicas(mine):
        return [mine] + [
            lax.ppermute(mine, "rep", [(i, (i + step) % replicas) for i in range(replicas)])
            for step in range(1, replicas)
        ]

    indices = from_replicas(comp_index[0][:, None])
    values = from_replicas(comp_value[0].astype(jnp.float32)[:, None])
    gate_f = gate_r.astype(jnp.float32)
    up_f = up_r.astype(jnp.float32)
    sigmoid_g = jax.nn.sigmoid(gate_f)
    activated = gate_f * sigmoid_g
    hidden = (activated * up_f).astype(jnp.bfloat16)
    summed = lax.psum_scatter(
        jnp.dot(hidden, down_weight, preferred_element_type=jnp.float32).astype(jnp.bfloat16),
        "tp",
        scatter_dimension=0,
        tiled=True,
    ).astype(jnp.float32)
    incoming = lax.all_gather(grads_r, "tp", axis=0, tiled=True)
    from_out = lax.dot_general(
        incoming, down_weight, (((1,), (1,)), ((), ())), preferred_element_type=jnp.float32
    )
    hidden_grad = from_out
    weight_sum = lax.dot_general(
        hidden, incoming, (((0,), (0,)), ((), ())), preferred_element_type=jnp.float32
    )
    weight_sum, hidden_grad = (weight_sum, hidden_grad)
    output = (residual_r.astype(jnp.float32) + summed).astype(jnp.bfloat16)
    gate_preact_gradient = (
        hidden_grad * up_f * sigmoid_g * (1.0 + gate_f * (1.0 - sigmoid_g))
    ).astype(jnp.bfloat16)
    up_grad = (hidden_grad * activated).astype(jnp.bfloat16)
    update, updated_down_weight = decode(indices, values, down_weight)
    return (
        output[None],
        gate_preact_gradient[None],
        up_grad[None],
        weight_sum.astype(jnp.bfloat16)[None],
        update,
        updated_down_weight,
    )


def solution(mesh):
    return jax.shard_map(
        shards,
        mesh=mesh,
        in_specs=(
            P("rep", "tp", None),
            P("rep", None, "tp"),
            P("rep", None, "tp"),
            P("tp", None),
            P("rep", "tp", None),
            P("rep", "tp", None),
            P("rep", "tp", None),
        ),
        out_specs=(
            P("rep", "tp", None),
            P("rep", None, "tp"),
            P("rep", None, "tp"),
            P("rep", "tp", None),
            P("tp", None),
            P("tp", None),
        ),
        check_vma=False,
    )
```

profile of v0, /device:TPU:0, one launch (start us, length us, event | category | flops | bytes accessed | tf_op | source)
XLA Modules:
  0.0 194.0 jit_solution(5593333141852051729)
XLA Ops:
  7.2 0.0 all-gather.3.cloned.1.call-start
  7.2 0.7 all-gather.3.cloned.1.call-update
  7.9 0.0 reduce-scatter.2.cloned.1.call-start
  7.9 14.8 %convolution_convert_fusion = bf16[1024,4096]{1,0:T(8,128)(2,1)} fusion(bf16[896,4096]{1,0:T(8,128)(2,1)} %refs_8_.1, bf16[1,1024,896]{2,1,0:T(8,128)(2,1)} %param.11, bf16[1,1024,896]{2,1,0:T(8,128)(2,1)} %param.10), kind=kOutput, calls=%fused_computation.4 | convolution fusion | flops 7527727104 | bytes 19398656 | tf_op jit(solution)/shard_map/dot_general | solution.py:123
  22.7 0.0 copy-start.6
  22.7 0.0 copy-start.2
  22.7 0.0 copy-start.3
  22.7 0.0 copy-start.4
  22.7 0.0 copy-start.7
  22.7 0.0 reduce-scatter.2.cloned.1.call-update
  22.8 0.8 copy-done.6
  23.6 0.1 bitcast_convert_fusion.refs_4_
  23.6 4.0 %collective-permute-start.5 = (f32[14,1,2048]{2,1,0:T(1,128)S(1)}, f32[14,1,2048]{2,1,0:T(1,128)S(1)}, u32[]{:S(2)}, u32[]{:S(2)}) collective-permute-start(f32[14,1,2048]{2,1,0:T(1,128)S(1)} %bitcast_convert_fusion.refs_4_), channel_id=1, source_target_pairs={{0,24},{8,0},{16,8},{24,16},{1,25},{9,1},{17,9},{25,17},{2,26},{10... | collective-permute-start | bytes 344072 | tf_op jit(solution)/shard_map/ppermute | solution.py:111
  27.6 0.5 collective-permute-start.4
  28.1 0.5 collective-permute-start.3
  28.7 0.0 copy-done.2
  28.7 2.4 %collective-permute-start.2 = (s32[14,1,2048]{2,1,0:T(1,128)S(1)}, s32[14,1,2048]{2,1,0:T(1,128)S(1)}, u32[]{:S(2)}, u32[]{:S(2)}) collective-permute-start(s32[14,1,2048]{2,1,0:T(1,128)S(1)} %bitcast.46), channel_id=1, source_target_pairs={{0,24},{8,0},{16,8},{24,16},{1,25},{9,1},{17,9},{25,17},{2,26},{10... | collective-permute-start | bytes 344072 | tf_op jit(solution)/shard_map/ppermute | solution.py:111
  31.1 1.5 collective-permute-start.1
  32.6 0.0 collective-permute-done.5.refs_7_
  32.6 1.0 collective-permute-start
  33.6 3.4 %collective-permute-done.4.refs_6_ = f32[14,1,2048]{2,1,0:T(1,128)S(1)} collective-permute-done((f32[14,1,2048]{2,1,0:T(1,128)S(1)}, f32[14,1,2048]{2,1,0:T(1,128)S(1)}, u32[]{:S(2)}, u32[]{:S(2)}) %collective-permute-start.4) | collective-permute-done | bytes 114720 | tf_op jit(solution)/shard_map/ppermute | solution.py:111
  37.0 0.0 collective-permute-done.3.refs_5_
  37.0 0.1 collective-permute-done.2.refs_3_
  37.1 2.5 %collective-permute-done.1.refs_2_ = s32[14,1,2048]{2,1,0:T(1,128)S(1)} collective-permute-done((s32[14,1,2048]{2,1,0:T(1,128)S(1)}, s32[14,1,2048]{2,1,0:T(1,128)S(1)}, u32[]{:S(2)}, u32[]{:S(2)}) %collective-permute-start.1) | collective-permute-done | bytes 114720 | tf_op jit(solution)/shard_map/ppermute | solution.py:111
  39.6 0.0 collective-permute-done.refs_1_
  39.6 0.0 copy-done.3
  39.6 0.0 copy-done.4
  39.7 0.0 copy-start
  39.7 3.1 %copy-done = bf16[896,4096]{1,0:T(8,128)(2,1)S(1)} copy-done((bf16[896,4096]{1,0:T(8,128)(2,1)S(1)}, bf16[896,4096]{1,0:T(8,128)(2,1)}, u32[]{:S(2)}) %copy-start) | copy-done | bytes 7340056
  42.7 34.5 %decode.1 = (bf16[896,4096]{1,0:T(8,128)(2,1)}, bf16[896,4096]{1,0:T(8,128)(2,1)}) custom-call(s32[14,1,2048]{2,1,0:T(1,128)S(1)} %bitcast.49, s32[14,1,2048]{2,1,0:T(1,128)S(1)} %collective-permute-done.refs_1_, s32[14,1,2048]{2,1,0:T(1,128)S(1)} %collective-permute-done.1.refs_2_, s32[14,1,2048]{2,1,0:T(1,128)S(1)} %collective-permute-done.2.refs_3_, ...), custom_call_target="tpu_custom_call" | custom-call | flops 20000000000 | bytes 22020096 | tf_op jit(solution)/shard_map/decode/pallas_call | solution.py:84
  77.3 17.1 %all-gather.3.cloned.1.call-done = bf16[1,1024,4096]{2,1,0:T(8,128)(2,1)} async-done(((bf16[1,128,4096]{2,1,0:T(8,128)(2,1)}), bf16[1,1024,4096]{2,1,0:T(8,128)(2,1)}) %all-gather.3.cloned.1.call-update) | async-done | bytes 8388624 | tf_op jit(solution)/shard_map/all_gather | solution.py:128
  94.4 0.0 copy-done.7
  94.4 0.0 copy-start.1
  94.4 0.0 copy-start.8
  94.4 13.3 %convert_bitcast_fusion = bf16[1,896,4096]{2,1,0:T(8,128)(2,1)} fusion(bf16[1,1024,4096]{2,1,0:T(8,128)(2,1)} %all-gather.3.cloned.1.call-done, bf16[1,1024,896]{2,1,0:T(8,128)(2,1)S(1)} %copy-done.7, bf16[1,1024,896]{2,1,0:T(8,128)(2,1)} %param.10), kind=kOutput, calls=%fused_computation.5 | convolution fusion | flops 7527202816 | bytes 19398656 | tf_op jit(solution)/shard_map/dot_general | solution.py:133
  107.7 0.0 copy-done.1
  107.7 0.0 copy-done.8
  107.7 0.0 copy-start.5
  107.7 13.8 %fusion.15 = (bf16[1,1024,896]{2,1,0:T(8,128)(2,1)}, bf16[1,1024,896]{2,1,0:T(8,128)(2,1)}) fusion(bf16[1,1024,896]{2,1,0:T(8,128)(2,1)S(1)} %copy-done.8, bf16[1,1024,896]{2,1,0:T(8,128)(2,1)S(1)} %copy-done.7, bf16[896,4096]{1,0:T(8,128)(2,1)S(1)} %copy-done.1, bf16[1,1024,4096]{2,1,0:T(8,128)(2,1)} %all-gather.3.cloned.1.call-done), kind=kOutput, calls=%fused_computation.22 | convolution fusion | flops 7529955328 | bytes 23068672 | tf_op jit(solution)/shard_map/dot_general | solution.py:129
  121.5 63.2 %reduce-scatter.2.cloned.1.call-done = bf16[128,4096]{1,0:T(8,128)(2,1)} async-done(((bf16[1024,4096]{1,0:T(8,128)(2,1)}), bf16[128,4096]{1,0:T(8,128)(2,1)}) %reduce-scatter.2.cloned.1.call-update) | async-done | bytes 1048592 | tf_op jit(solution)/shard_map/reduce_scatter | solution.py:122
  184.7 0.0 copy-done.5
  184.7 2.4 %fusion.17 = bf16[1,128,4096]{2,1,0:T(8,128)(2,1)} fusion(bf16[128,4096]{1,0:T(8,128)(2,1)} %reduce-scatter.2.cloned.1.call-done, bf16[1,128,4096]{2,1,0:T(8,128)(2,1)S(1)} %copy-done.5), kind=kLoop, calls=%fused_computation.24 | loop fusion | flops 2097152 | bytes 3145728 | tf_op jit(solution)/shard_map/broadcast_in_dim | solution.py:144
Async XLA Ops:
  7.2 87.2 %all-gather.3.cloned.1.call-start = ((), (), s32[]{:S(2)}) async-start(), calls=%async_computation.2 | async-start | bytes 9437184 | tf_op jit(solution)/shard_map/all_gather | solution.py:128
  7.9 176.8 %reduce-scatter.2.cloned.1.call-start = ((), (), s32[]{:S(2)}) async-start(), calls=%async_computation.1 | async-start | bytes 9437184 | tf_op jit(solution)/shard_map/reduce_scatter | solution.py:122
  22.7 0.8 copy-start.6
  22.7 5.9 %copy-start.2 = (s32[1,14,2048]{2,0,1:T(1,128)S(1)}, s32[1,14,2048]{2,0,1:T(1,128)}, u32[]{:S(2)}) copy-start(s32[1,14,2048]{2,0,1:T(1,128)} %param.14) | copy-start | bytes 344068
  22.7 16.9 %copy-start.3 = (bf16[256,256]{1,0:T(8,128)(2,1)S(1)}, bf16[256,256]{1,0:T(8,128)(2,1)}, u32[]{:S(2)}) copy-start(bf16[256,256]{1,0:T(8,128)(2,1)} %constant.6.clone.refs_9_) | copy-start | bytes 393220
  22.7 16.9 %copy-start.4 = (bf16[64,64]{1,0:T(8,128)(2,1)S(1)}, bf16[64,64]{1,0:T(8,128)(2,1)}, u32[]{:S(2)}) copy-start(bf16[64,64]{1,0:T(8,128)(2,1)} %constant.7.clone.refs_10_) | copy-start | bytes 24580
  22.7 71.6 %copy-start.7 = (bf16[1,1024,896]{2,1,0:T(8,128)(2,1)S(1)}, bf16[1,1024,896]{2,1,0:T(8,128)(2,1)}, u32[]{:S(2)}) copy-start(bf16[1,1024,896]{2,1,0:T(8,128)(2,1)} %param.11) | copy-start | bytes 5505028
  23.6 8.9 %collective-permute-start.5 = (f32[14,1,2048]{2,1,0:T(1,128)S(1)}, f32[14,1,2048]{2,1,0:T(1,128)S(1)}, u32[]{:S(2)}, u32[]{:S(2)}) collective-permute-start(f32[14,1,2048]{2,1,0:T(1,128)S(1)} %bitcast_convert_fusion.refs_4_), channel_id=1, source_target_pairs={{0,24},{8,0},{16,8},{24,16},{1,25},{9,1},{17,9},{25,17},{2,26},{10... | collective-permute-start | bytes 344072 | tf_op jit(solution)/shard_map/ppermute | solution.py:111
  27.6 9.4 %collective-permute-start.4 = (f32[14,1,2048]{2,1,0:T(1,128)S(1)}, f32[14,1,2048]{2,1,0:T(1,128)S(1)}, u32[]{:S(2)}, u32[]{:S(2)}) collective-permute-start(f32[14,1,2048]{2,1,0:T(1,128)S(1)} %bitcast_convert_fusion.refs_4_), channel_id=1, source_target_pairs={{0,16},{8,24},{16,0},{24,8},{1,17},{9,25},{17,1},{25,9},{2,18},{10... | collective-permute-start | bytes 344072 | tf_op jit(solution)/shard_map/ppermute | solution.py:111
  28.1 8.9 %collective-permute-start.3 = (f32[14,1,2048]{2,1,0:T(1,128)S(1)}, f32[14,1,2048]{2,1,0:T(1,128)S(1)}, u32[]{:S(2)}, u32[]{:S(2)}) collective-permute-start(f32[14,1,2048]{2,1,0:T(1,128)S(1)} %bitcast_convert_fusion.refs_4_), channel_id=1, source_target_pairs={{0,8},{8,16},{16,24},{24,0},{1,9},{9,17},{17,25},{25,1},{2,10},{10... | collective-permute-start | bytes 344072 | tf_op jit(solution)/shard_map/ppermute | solution.py:111
  28.7 8.5 %collective-permute-start.2 = (s32[14,1,2048]{2,1,0:T(1,128)S(1)}, s32[14,1,2048]{2,1,0:T(1,128)S(1)}, u32[]{:S(2)}, u32[]{:S(2)}) collective-permute-start(s32[14,1,2048]{2,1,0:T(1,128)S(1)} %bitcast.46), channel_id=1, source_target_pairs={{0,24},{8,0},{16,8},{24,16},{1,25},{9,1},{17,9},{25,17},{2,26},{10... | collective-permute-start | bytes 344072 | tf_op jit(solution)/shard_map/ppermute | solution.py:111
  31.1 8.6 %collective-permute-start.1 = (s32[14,1,2048]{2,1,0:T(1,128)S(1)}, s32[14,1,2048]{2,1,0:T(1,128)S(1)}, u32[]{:S(2)}, u32[]{:S(2)}) collective-permute-start(s32[14,1,2048]{2,1,0:T(1,128)S(1)} %bitcast.47), channel_id=1, source_target_pairs={{0,16},{8,24},{16,0},{24,8},{1,17},{9,25},{17,1},{25,9},{2,18},{10... | collective-permute-start | bytes 344072 | tf_op jit(solution)/shard_map/ppermute | solution.py:111
  32.6 7.1 %collective-permute-start = (s32[14,1,2048]{2,1,0:T(1,128)S(1)}, s32[14,1,2048]{2,1,0:T(1,128)S(1)}, u32[]{:S(2)}, u32[]{:S(2)}) collective-permute-start(s32[14,1,2048]{2,1,0:T(1,128)S(1)} %bitcast.48), channel_id=1, source_target_pairs={{0,8},{8,16},{16,24},{24,0},{1,9},{9,17},{17,25},{25,1},{2,10},{10... | collective-permute-start | bytes 344072 | tf_op jit(solution)/shard_map/ppermute | solution.py:111
  39.7 3.1 %copy-start = (bf16[896,4096]{1,0:T(8,128)(2,1)S(1)}, bf16[896,4096]{1,0:T(8,128)(2,1)}, u32[]{:S(2)}) copy-start(bf16[896,4096]{1,0:T(8,128)(2,1)} %refs_8_.1) | copy-start | bytes 22020100
  94.4 13.3 %copy-start.1 = (bf16[896,4096]{1,0:T(8,128)(2,1)S(1)}, bf16[896,4096]{1,0:T(8,128)(2,1)}, u32[]{:S(2)}) copy-start(bf16[896,4096]{1,0:T(8,128)(2,1)} %refs_8_.1) | copy-start | bytes 22020100
  94.4 13.3 %copy-start.8 = (bf16[1,1024,896]{2,1,0:T(8,128)(2,1)S(1)}, bf16[1,1024,896]{2,1,0:T(8,128)(2,1)}, u32[]{:S(2)}) copy-start(bf16[1,1024,896]{2,1,0:T(8,128)(2,1)} %param.10) | copy-start | bytes 5505028
  107.7 77.0 %copy-start.5 = (bf16[1,128,4096]{2,1,0:T(8,128)(2,1)S(1)}, bf16[1,128,4096]{2,1,0:T(8,128)(2,1)}, u32[]{:S(2)}) copy-start(bf16[1,128,4096]{2,1,0:T(8,128)(2,1)} %param.9) | copy-start | bytes 3145732
Sparse Core Ops, SparseCore 0:
  9.6 84.7 all-gather.2
  96.7 88.0 reduce-scatter.1
where the time goes:
time: 194 us
  waiting for transfers between devices  87.1 us (45%)
  matrix products  41.8 us (22%)
  Pallas kernels  34.5 us (18%)
  between operations  14.1 us (7%)
  starting transfers between devices  10 us (5%)
  local copies, waits for them, and re-layouts  3.9 us (2%)
  other arithmetic  2.53 us (1%)
    reduce_scatter x1, waiting for transfers between devices, shards(): lax.psum_scatter(jnp.dot(hidden, down_weight, preferred_element_type=jnp....  63.2 us
    pallas_call x1, Pallas kernels, decode(): pl.pallas_call(functools.partial(decode_kernel, count), grid=(span_rows,)...  34.5 us
    all_gather x1, waiting for transfers between devices, shards(): incoming = lax.all_gather(grads_r, 'tp', axis=0, tiled=True)  17.1 us
    dot_general x1, matrix products, shards(): jnp.dot(hidden, down_weight, preferred_element_type=jnp.float32)  14.8 us
    dot_general x1, matrix products, shards(): lax.dot_general(incoming, down_weight, (((1,), (1,)), ((), ())), preferre...  13.8 us
    dot_general x1, matrix products, shards(): lax.dot_general(hidden, incoming, (((0,), (0,)), ((), ())), preferred_ele...  13.3 us
    ppermute x6, starting transfers between devices, from_replicas(): lax.ppermute(mine, 'rep', [(i, (i + step) % replicas) for i in range(repl...  9.93 us
    ppermute x6, waiting for transfers between devices, from_replicas(): lax.ppermute(mine, 'rep', [(i, (i + step) % replicas) for i in range(repl...  6.06 us
  transfers between devices with their start and end apart: 8, of which 5 were waited for; matrix products, arithmetic and copies ran while one was open for 22% of the time, Pallas kernels for 18%

commit v1 on v0

--- a/solution.py
+++ b/solution.py
@@ -16,6 +16,10 @@
 
 
 LANES = 128
+UNROLL = 4
+MESH = pl.DeviceIdType.MESH
+VMEM_BYTES = 66_000_000
+CHUNKS = 4
 
 
 def cosine_table(length):
@@ -67,18 +71,20 @@
         ).astype(jnp.bfloat16)
 
 
-UNROLL = 4
+def decode_tables():
+    basis = cosine_table(SPAN)
+    right = jnp.asarray(np.kron(np.eye(LANES // TOPK), basis), jnp.bfloat16)
+    left = jnp.asarray(basis.T, jnp.bfloat16)
+    return right, left
 
 
 def decode(indices, values, down_weight):
     count = len(indices)
     span_rows, _, listed = indices[0].shape
     units, model = down_weight.shape
-    basis = cosine_table(SPAN)
     per_group = LANES // TOPK
     width = per_group * SPAN
-    right = jnp.asarray(np.kron(np.eye(per_group), basis), jnp.bfloat16)
-    left = jnp.asarray(basis.T, jnp.bfloat16)
+    right, left = decode_tables()
     strip = pl.BlockSpec((SPAN, model), lambda a: (a, 0))
     whole = lambda shape: pl.BlockSpec(shape, lambda a: (0, 0))
     return pl.pallas_call(
@@ -99,11 +105,7 @@
     )(*indices, *values, down_weight, right, left)
 
 
-def shards(residual, gate_pre, up_pre, down_weight, d_out, comp_index, comp_value):
-    residual_r = residual[0]
-    gate_r = gate_pre[0]
-    up_r = up_pre[0]
-    grads_r = d_out[0]
+def plain_shards(residual_r, gate_r, up_r, down_weight, grads_r, index_r, value_r):
     replicas = lax.axis_size("rep")
 
     def from_replicas(mine):
@@ -112,8 +114,8 @@
             for step in range(1, replicas)
         ]
 
-    indices = from_replicas(comp_index[0][:, None])
-    values = from_replicas(comp_value[0].astype(jnp.float32)[:, None])
+    indices = from_replicas(index_r[:, None])
+    values = from_replicas(value_r.astype(jnp.float32)[:, None])
     gate_f = gate_r.astype(jnp.float32)
     up_f = up_r.astype(jnp.float32)
     sigmoid_g = jax.nn.sigmoid(gate_f)
@@ -126,27 +128,503 @@
         tiled=True,
     ).astype(jnp.float32)
     incoming = lax.all_gather(grads_r, "tp", axis=0, tiled=True)
-    from_out = lax.dot_general(
+    hidden_grad = lax.dot_general(
         incoming, down_weight, (((1,), (1,)), ((), ())), preferred_element_type=jnp.float32
     )
-    hidden_grad = from_out
     weight_sum = lax.dot_general(
         hidden, incoming, (((0,), (0,)), ((), ())), preferred_element_type=jnp.float32
     )
-    weight_sum, hidden_grad = (weight_sum, hidden_grad)
     output = (residual_r.astype(jnp.float32) + summed).astype(jnp.bfloat16)
     gate_preact_gradient = (
         hidden_grad * up_f * sigmoid_g * (1.0 + gate_f * (1.0 - sigmoid_g))
     ).astype(jnp.bfloat16)
     up_grad = (hidden_grad * activated).astype(jnp.bfloat16)
     update, updated_down_weight = decode(indices, values, down_weight)
+    return output, gate_preact_gradient, up_grad, weight_sum.astype(jnp.bfloat16), update, updated_down_weight
+
+
+def rows_at(start, size):
+    return pl.ds(pl.multiple_of(start, size), size)
+
+
+def joint_kernel(
+    n, replicas,
+    residual, gate, up, weight, grads, index, value, right_ref, left_ref,
+    output, gate_grad, up_grad, weight_grad, update, updated,
+    dall, slot_up, slot_dn, part, peer, w_v, hidden, hidden_t, gate_v, up_v, res_v,
+    index_v, value_v, row_v, col_v, amount_v, mixed, upd_st, new_st, gg_st, ug_st, wg_st, fin,
+    load_sem, comp_send, comp_recv, step_send, step_recv, chip_send, chip_recv,
+    part_send, part_recv, upd_sem, new_sem, gg_sem, ug_sem, wg_sem, out_sem,
+):
+    chips = n // 2
+    rep = lax.axis_index("rep")
+    me = lax.axis_index("tp")
+    z, core = me // 2, me % 2
+    partner = me + 1 - 2 * core
+    tokens, units = gate_v.shape
+    model = w_v.shape[1]
+    block = tokens // n
+    piece = block // CHUNKS
+    span_rows, listed = index_v.shape[1], index_v.shape[2]
+    groups = listed // LANES
+    per_group = LANES // TOPK
+    width = per_group * SPAN
+    f32, bf16 = jnp.float32, jnp.bfloat16
+
+    def cond(pred):
+        return pl.when(pred)
+
+    loads = [
+        pltpu.make_async_copy(gate, gate_v, load_sem.at[0]),
+        pltpu.make_async_copy(up, up_v, load_sem.at[1]),
+        pltpu.make_async_copy(weight, w_v, load_sem.at[2]),
+        pltpu.make_async_copy(grads, dall.at[rows_at(me * block, block)], load_sem.at[3]),
+        pltpu.make_async_copy(index, index_v.at[rep], load_sem.at[4]),
+        pltpu.make_async_copy(value, value_v.at[rep], load_sem.at[5]),
+        pltpu.make_async_copy(residual, res_v, load_sem.at[6]),
+    ]
+    for load in loads:
+        load.start()
+
+    barrier = pltpu.get_barrier_semaphore()
+    has_up, has_dn = z < chips - 1, z > 0
+
+    @cond(has_up)
+    def _():
+        pl.semaphore_signal(barrier, inc=1, device_id={"tp": me + 2}, device_id_type=MESH)
+
+    @cond(has_dn)
+    def _():
+        pl.semaphore_signal(barrier, inc=1, device_id={"tp": me - 2}, device_id_type=MESH)
+
+    pl.semaphore_signal(barrier, inc=1, device_id={"tp": partner}, device_id_type=MESH)
+    for step in range(1, replicas):
+        pl.semaphore_signal(
+            barrier, inc=1, device_id={"rep": (rep + step) % replicas}, device_id_type=MESH
+        )
+    pl.semaphore_wait(barrier, replicas + has_up.astype(jnp.int32) + has_dn.astype(jnp.int32))
+
+    def send(way, s, src, dst):
+        return pltpu.make_async_remote_copy(
+            src_ref=src, dst_ref=dst, send_sem=step_send.at[way, s], recv_sem=step_recv.at[way, s],
+            device_id={"tp": me + (2 if way == 0 else -2)}, device_id_type=MESH,
+        )
+
+    def grad_piece(chip, q):
+        return dall.at[rows_at((2 * chip + core) * block + q * piece, piece)]
+
+    def to_partner(chip, q):
+        return pltpu.make_async_remote_copy(
+            src_ref=grad_piece(chip, q), dst_ref=grad_piece(chip, q),
+            send_sem=chip_send.at[chip * CHUNKS + q], recv_sem=chip_recv.at[chip * CHUNKS + q],
+            device_id={"tp": partner}, device_id_type=MESH,
+        )
+
+    def hand_over(target):
+        return pltpu.make_async_remote_copy(
+            src_ref=part.at[rows_at((2 * target + 1 - core) * block, block)],
+            dst_ref=peer.at[rows_at(target * block, block)],
+            send_sem=part_send.at[target], recv_sem=part_recv.at[target],
+            device_id={"tp": partner}, device_id_type=MESH,
+        )
+
+    def comp_copies(step):
+        to = {"rep": (rep + step) % replicas}
+        return [
+            pltpu.make_async_remote_copy(
+                src_ref=src, dst_ref=dst.at[rep], send_sem=comp_send.at[kind, step - 1],
+                recv_sem=comp_recv.at[kind, step - 1], device_id=to, device_id_type=MESH,
+            )
+            for kind, (src, dst) in enumerate(((index, index_v), (value, value_v)))
+        ]
+
+    slots = (slot_up, slot_dn)
+    rank = (z, chips - 1 - z)
+    onward = (has_up, has_dn)
+    behind = (has_dn, has_up)
+
+    for q in range(CHUNKS):
+        for way in range(2):
+            @cond(onward[way])
+            def _():
+                send(way, q, grads.at[pl.ds(q * piece, piece)], grad_piece(z, q)).start()
+
+    for step in range(1, replicas):
+        for copy in comp_copies(step):
+            copy.start()
+
+    loads[3].wait()
+    for q in range(CHUNKS):
+        to_partner(z, q).start()
+
+    def own_sum(target, q):
+        mine = part[rows_at((2 * target + core) * block + q * piece, piece), :].astype(f32)
+        other = peer[rows_at(target * block + q * piece, piece), :].astype(f32)
+        return mine + other
+
+    def slot_rows(p, q):
+        return rows_at((p - 1) * block + q * piece, piece)
+
+    def service(s):
+        p, q = s // CHUNKS, s % CHUNKS
+        for way in range(2):
+            at, slot = rank[way], slots[way]
+            gathered = p < at
+            source = z - 1 - p if way == 0 else z + 1 + p
+            target = chips + z - 1 - p if way == 0 else z - chips + 1 + p
+            summing = jnp.logical_and(jnp.logical_and(p >= at, onward[way]), p < chips - 1)
+            first = at == 0
+
+            @cond(behind[way])
+            def _():
+                send(way, s, grad_piece(z, q), grad_piece(z, q)).wait_recv()
+
+            @cond(gathered)
+            def _():
+                to_partner(source, q).start()
+
+                @cond(onward[way])
+                def _():
+                    send(way, s + CHUNKS, grad_piece(source, q), grad_piece(source, q)).start()
+
+            @cond(jnp.logical_and(summing, first))
+            def _():
+                slot[slot_rows(p + 1, q), :] = own_sum(target, q).astype(bf16)
+                send(way, s + CHUNKS, slot.at[slot_rows(p + 1, q)], slot.at[slot_rows(p + 1, q)]).start()
+
+            @cond(jnp.logical_and(summing, jnp.logical_not(first)))
+            def _():
+                here = slot_rows(p, q)
+                slot[here, :] = (own_sum(target, q) + slot[here, :].astype(f32)).astype(bf16)
+                send(way, s + CHUNKS, slot.at[here], slot.at[slot_rows(p + 1, q)]).start()
+
+    def put_output(q):
+        return pltpu.make_async_copy(fin_b.at[pl.ds(q * piece, piece)], output.at[pl.ds(q * piece, piece)], out_sem.at[q])
+
+    fin_b = res_v
+
+    def finish(q):
+        here = pl.ds(q * piece, piece)
+        fin[...] = res_v[here, :].astype(f32) + own_sum(z, q)
+        for way in range(2):
+            @cond(behind[way])
+            def _():
+                fin[...] = fin[...] + slots[way][pl.ds((chips - 2) * block + q * piece, piece), :].astype(f32)
+        res_v[here, :] = fin[...].astype(bf16)
+        put_output(q).start()
+
+    loads[0].wait()
+    loads[1].wait()
+
+    def make_hidden(i, carry):
+        here = rows_at(i * LANES, LANES)
+        g = gate_v[here, :].astype(f32)
+        u = up_v[here, :].astype(f32)
+        h = (g * jax.nn.sigmoid(g) * u).astype(bf16)
+        hidden[here, :] = h
+        hidden_t[:, here] = h.astype(f32).T.astype(bf16)
+        return carry
+
+    lax.fori_loop(0, tokens // LANES, make_hidden, 0)
+
+    loads[2].wait()
+    tile = 512
+
+    def make_part(i, carry):
+        here = rows_at(i * tile, tile)
+        part[:, here] = jnp.dot(hidden[...], w_v[:, here], preferred_element_type=f32).astype(bf16)
+        return carry
+
+    lax.fori_loop(0, model // tile, make_part, 0)
+    order = []
+    for k in range(chips):
+        order.append(chips - 1 - k // 2 if k % 2 == 0 else k // 2)
+    for target in order:
+        hand_over(target).start()
+
+    for step in range(1, replicas):
+        for copy in comp_copies(step):
+            copy.wait_recv()
+    loads[4].wait()
+    loads[5].wait()
+    pairs = replicas // 2
+    half = LANES // 2
+    spot = lax.broadcasted_iota(jnp.int32, (span_rows, listed), 1)
+    lower = spot % LANES < half
+    shift = ((spot // TOPK) % 2) * SPAN
+
+    def spread_out(dest, arrays):
+        for j in range(pairs):
+            even, odd = arrays[2 * j], arrays[2 * j + 1]
+            first = jnp.where(lower, even, pltpu.roll(odd, half, 1))
+            second = jnp.where(lower, pltpu.roll(even, listed - half, 1), odd)
+            for a in range(span_rows):
+                dest[a, j:j + 1, :] = first[a:a + 1]
+                dest[a, pairs + j:pairs + j + 1, :] = second[a:a + 1]
+
+    spread_out(row_v, [(index_v[r] >> (SPAN.bit_length() - 1)).astype(f32) for r in range(replicas)])
+    spread_out(col_v, [((index_v[r] & (SPAN - 1)) + shift).astype(f32) for r in range(replicas)])
+    spread_out(amount_v, [value_v[r].astype(f32) for r in range(replicas)])
+    deep = pairs * LANES
+    row_place = lax.broadcasted_iota(jnp.int32, (SPAN, deep), 0).astype(f32).astype(bf16)
+    col_place = lax.broadcasted_iota(jnp.int32, (2 * SPAN, deep), 0).astype(f32).astype(bf16)
+
+    def put_update(a, k):
+        rows = rows_at(a * SPAN, SPAN)
+        return (
+            pltpu.make_async_copy(upd_st.at[k], update.at[rows], upd_sem.at[k]),
+            pltpu.make_async_copy(new_st.at[k], updated.at[rows], new_sem.at[k]),
+        )
+
+    def decode_row(a):
+        k = a % 2
+
+        @cond(a >= 2)
+        def _():
+            for copy in put_update(a, k):
+                copy.wait()
+
+        def gather(group, carry):
+            at = rows_at(group * LANES, LANES)
+            row_set, col_set, amount_set = row_v[a, :, at], col_v[a, :, at], amount_v[a, :, at]
+            for side in range(2):
+                line = lambda x: jnp.concatenate(
+                    [x[side * pairs + j:side * pairs + j + 1] for j in range(pairs)], axis=1
+                ).astype(bf16)
+                row_hot = jnp.where(line(row_set) == row_place, line(amount_set), bf16(0))
+                col_hot = jnp.where(line(col_set) == col_place, bf16(1), bf16(0))
+                spectral = lax.dot_general(
+                    row_hot, col_hot, (((1,), (1,)), ((), ())), preferred_element_type=f32
+                )
+                mixed[rows_at(group * SPAN, SPAN), side * 2 * SPAN:(side + 1) * 2 * SPAN] = spectral.astype(bf16)
+            return carry
+
+        lax.fori_loop(0, groups, gather, 0, unroll=UNROLL)
+        halfway = jnp.dot(mixed[...], right_ref[...], preferred_element_type=f32).astype(bf16)
+        for group in range(groups):
+            spread = jnp.dot(
+                left_ref[...], halfway[group * SPAN:(group + 1) * SPAN], preferred_element_type=f32
+            )
+            change = (spread * (1.0 / replicas)).astype(bf16)
+            at = slice(group * width, (group + 1) * width)
+            upd_st[k, :, at] = change
+            new_st[k, :, at] = (
+                w_v[rows_at(a * SPAN, SPAN), at].astype(f32) - learn_rate * change.astype(f32)
+            ).astype(bf16)
+        for copy in put_update(a, k):
+            copy.start()
+
+    early = CHUNKS - 1
+    decode_head = 2
+
+    def decode_step(a, carry):
+        decode_row(a)
+
+        @cond(a == decode_head - 1)
+        def _():
+            for target in order:
+                hand_over(target).wait_recv()
+            for s in range(early):
+                service(s)
+
+        @cond(jnp.logical_and(a >= decode_head, a % 2 == 1))
+        def _():
+            service(early + (a - decode_head) // 2)
+
+        return carry
+
+    lax.fori_loop(0, span_rows, decode_step, 0)
+    served = early + (span_rows - decode_head) // 2
+    for k in range(2):
+        for copy in put_update(span_rows - 2 + k, k):
+            copy.wait()
+
+    def serve_to(start, stop):
+        if stop > start:
+            lax.fori_loop(start, stop, lambda s, carry: (service(s), carry)[1], 0)
+
+    low = z < chips // 2
+
+    def put_grads(start, k):
+        rows = rows_at(start, 2 * block)
+        return (
+            pltpu.make_async_copy(gg_st.at[k], gate_grad.at[rows], gg_sem.at[k]),
+            pltpu.make_async_copy(ug_st.at[k], up_grad.at[rows], ug_sem.at[k]),
+        )
+
+    def wait_chip(chip):
+        for q in range(CHUNKS):
+            to_partner(chip, q).wait_recv()
+
+    def chip_at(k):
+        return jnp.where(low, k, chips - 1 - k)
+
+    def grads_of(k, carry):
+        chip = chip_at(k)
+        start = chip * 2 * block
+        wait_chip(chip)
+        j = k % 2
+
+        @cond(k >= 2)
+        def _():
+            for copy in put_grads(start, j):
+                copy.wait()
+
+        rows = rows_at(start, 2 * block)
+        back = lax.dot_general(
+            dall[rows, :], w_v[...], (((1,), (1,)), ((), ())), preferred_element_type=f32
+        )
+        g = gate_v[rows, :].astype(f32)
+        u = up_v[rows, :].astype(f32)
+        sig = jax.nn.sigmoid(g)
+        gg_st[j] = (back * u * sig * (1.0 + g * (1.0 - sig))).astype(bf16)
+        ug_st[j] = (back * (g * sig)).astype(bf16)
+        for copy in put_grads(start, j):
+            copy.start()
+        return carry
+
+    serve_to(served, 2 * CHUNKS + 1)
+    lax.fori_loop(0, chips // 2, grads_of, 0)
+    serve_to(2 * CHUNKS + 1, (chips - 1) * CHUNKS)
+    lax.fori_loop(chips // 2, chips, grads_of, 0)
+
+    wide = 256
+    last = (chips - 1) * CHUNKS
+    service(last)
+    loads[6].wait()
+    finish(0)
+
+    def put_weight(i, k):
+        return pltpu.make_async_copy(wg_st.at[k], weight_grad.at[:, rows_at(i * wide, wide)], wg_sem.at[k])
+
+    def make_weight(i, carry):
+        k = i % 2
+
+        @cond(i >= 2)
+        def _():
+            put_weight(i, k).wait()
+
+        wg_st[k] = jnp.dot(
+            hidden_t[...], dall[:, rows_at(i * wide, wide)], preferred_element_type=f32
+        ).astype(bf16)
+        put_weight(i, k).start()
+        return carry
+
+    turns = model // wide
+    marks = [turns * k // (CHUNKS - 1) for k in range(CHUNKS)]
+    for q in range(1, CHUNKS):
+        lax.fori_loop(marks[q - 1], marks[q], make_weight, 0)
+        service(last + q)
+        finish(q)
+
+    for k in range(2):
+        put_weight(turns - 2 + k, k).wait()
+        for copy in put_grads(0, k):
+            copy.wait()
+    for q in range(CHUNKS):
+        put_output(q).wait()
+    for target in range(chips):
+        hand_over(target).wait_send()
+    for chip in range(chips):
+        for q in range(CHUNKS):
+            to_partner(chip, q).wait_send()
+    for step in range(1, replicas):
+        for copy in comp_copies(step):
+            copy.wait_send()
+    for way in range(2):
+        @cond(onward[way])
+        def _():
+            for s in range(chips * CHUNKS):
+                send(way, s, grad_piece(z, 0), grad_piece(z, 0)).wait_send()
+
+
+def joint_scratch(n, replicas, tokens, units, model, span_rows, listed):
+    chips, block = n // 2, tokens // n
+    bf16, f32 = jnp.bfloat16, jnp.float32
+    dma = pltpu.SemaphoreType.DMA
+    arrays = [
+        ((tokens, model), bf16),
+        (((chips - 1) * block, model), bf16),
+        (((chips - 1) * block, model), bf16),
+        ((tokens, model), bf16),
+        ((chips * block, model), bf16),
+        ((units, model), bf16),
+        ((tokens, units), bf16),
+        ((units, tokens), bf16),
+        ((tokens, units), bf16),
+        ((tokens, units), bf16),
+        ((block, model), bf16),
+        ((replicas, span_rows, listed), jnp.int32),
+        ((replicas, span_rows, listed), bf16),
+        ((span_rows, replicas, listed), f32),
+        ((span_rows, replicas, listed), f32),
+        ((span_rows, replicas, listed), f32),
+        ((listed // LANES * SPAN, LANES // TOPK * SPAN), bf16),
+        ((2, SPAN, model), bf16),
+        ((2, SPAN, model), bf16),
+        ((2, 2 * block, units), bf16),
+        ((2, 2 * block, units), bf16),
+        ((2, units, 256), bf16),
+        ((block // CHUNKS, model), f32),
+    ]
+    total = sum(int(np.prod(shape)) * jnp.dtype(kind).itemsize for shape, kind in arrays)
+    steps = chips * CHUNKS
+    sems = [
+        dma((7,)), dma((2, replicas - 1)), dma((2, replicas - 1)), dma((2, steps)), dma((2, steps)),
+        dma((steps,)), dma((steps,)), dma((chips,)), dma((chips,)),
+        dma((2,)), dma((2,)), dma((2,)), dma((2,)), dma((2,)), dma((CHUNKS,)),
+    ]
+    return total, [pltpu.VMEM(shape, kind) for shape, kind in arrays] + sems
+
+
+def joint(residual_r, gate_r, up_r, down_weight, grads_r, index_r, value_r, scratch):
+    n, replicas = lax.axis_size("tp"), lax.axis_size("rep")
+    (tokens, units), model = gate_r.shape, down_weight.shape[1]
+    right, left = decode_tables()
+    any_spec = pl.BlockSpec(memory_space=pl.ANY)
+    vmem_spec = pl.BlockSpec(memory_space=pltpu.VMEM)
+    shape = lambda *dims: jax.ShapeDtypeStruct(dims, jnp.bfloat16)
+    return pl.pallas_call(
+        functools.partial(joint_kernel, n, replicas),
+        out_shape=[
+            shape(*residual_r.shape), shape(tokens, units), shape(tokens, units),
+            shape(units, model), shape(units, model), shape(units, model),
+        ],
+        in_specs=[any_spec] * 7 + [vmem_spec] * 2,
+        out_specs=[any_spec] * 6,
+        scratch_shapes=scratch,
+        compiler_params=pltpu.CompilerParams(
+            collective_id=0, has_side_effects=True, vmem_limit_bytes=VMEM_BYTES
+        ),
+        cost_estimate=pl.CostEstimate(
+            flops=6 * tokens * units * model, bytes_accessed=units * model * 8, transcendentals=0
+        ),
+        name="joint",
+    )(residual_r, gate_r, up_r, down_weight, grads_r, index_r, value_r, right, left)
+
+
+def shards(residual, gate_pre, up_pre, down_weight, d_out, comp_index, comp_value):
+    operands = (residual[0], gate_pre[0], up_pre[0], down_weight, d_out[0], comp_index[0], comp_value[0])
+    n, replicas = lax.axis_size("tp"), lax.axis_size("rep")
+    tokens, units = gate_pre.shape[1:]
+    span_rows, listed = comp_index.shape[1:]
+    model = down_weight.shape[1]
+    fits = False
+    if n % 4 == 0 and units % LANES == 0 and span_rows % 2 == 0 and replicas % 2 == 0:
+        total, scratch = joint_scratch(n, replicas, tokens, units, model, span_rows, listed)
+        fits = total < 56 * 2**20 and n // 2 == CHUNKS
+    if fits:
+        outs = joint(*operands, scratch)
+    else:
+        outs = plain_shards(*operands)
+    output, gate_preact_gradient, up_grad, weight_sum, update, updated = outs
     return (
         output[None],
         gate_preact_gradient[None],
         up_grad[None],
-        weight_sum.astype(jnp.bfloat16)[None],
+        weight_sum[None],
         update,
-        updated_down_weight,
+        updated,
     )
 
 

time: 194 us -> 124 us (0.64)
  waiting for transfers between devices: 87.1 us -> 0 us
  Pallas kernels: 34.5 us -> 99.1 us
  matrix products: 41.8 us -> 0 us
  local copies, waits for them, and re-layouts: 3.9 us -> 24.2 us
  between operations: 14.1 us -> 0.65 us
  starting transfers between devices: 10 us -> 0 us
  other arithmetic: 2.53 us -> 0.01 us
    pallas_call x1, Pallas kernels: 34.5 us -> 99.1 us  [joint(): pl.pallas_call(functools.partial(joint_kernel, n, replicas), out_shape=[s...]
    reduce_scatter x1 -> x0, waiting for transfers between devices: 63.2 us -> none  [shards(): lax.psum_scatter(jnp.dot(hidden, down_weight, preferred_element_type=jnp....]
    dot_general x3 -> x0, matrix products: 41.8 us -> none  [the longest x1 14.8 us: shards(): jnp.dot(hidden, down_weight, preferred_element_type=jnp.float32)]
    unnamed x18 -> x13, local copies, waits for them, and re-layouts: 3.9 us -> 24.2 us
    all_gather x1 -> x0, waiting for transfers between devices: 17.1 us -> none  [shards(): incoming = lax.all_gather(grads_r, 'tp', axis=0, tiled=True)]
    ppermute x6 -> x0, starting transfers between devices: 9.93 us -> none  [from_replicas(): lax.ppermute(mine, 'rep', [(i, (i + step) % replicas) for i in range(repl...]
    ppermute x6 -> x0, waiting for transfers between devices: 6.06 us -> none  [from_replicas(): lax.ppermute(mine, 'rep', [(i, (i + step) % replicas) for i in range(repl...]
    broadcast_in_dim x1 -> x0, other arithmetic: 2.44 us -> none  [shards(): output[None]]
  transfers between devices with their start and end apart: 8 -> 0, of which waited for: 5 -> 0; matrix products, arithmetic and copies ran while one was open for 22% -> 0% of each run, Pallas kernels for 18% -> 0%
where the time goes in v1:
time: 124 us
  Pallas kernels  99.1 us (80%)
  local copies, waits for them, and re-layouts  24.2 us (20%)
    pallas_call x1, Pallas kernels, joint(): pl.pallas_call(functools.partial(joint_kernel, n, replicas), out_shape=[s...  99.1 us
    unnamed x13, local copies, waits for them, and re-layouts  24.2 us

profile of v1, /device:TPU:0, one launch (start us, length us, event | category | flops | bytes accessed | tf_op | source)
XLA Modules:
  0.0 123.9 jit_solution(10637121641702440451)
XLA Ops:
  0.6 1.6 %copy.17 = s32[1,14,2048]{2,1,0:T(8,128)} copy(s32[1,14,2048]{2,0,1:T(1,128)} %param.14) | data formatting | bytes 229376
  2.2 99.1 %joint.1 = (bf16[128,4096]{1,0:T(8,128)(2,1)}, bf16[1024,896]{1,0:T(8,128)(2,1)}, bf16[1024,896]{1,0:T(8,128)(2,1)}, bf16[896,4096]{1,0:T(8,128)(2,1)}, bf16[896...) custom-call(bf16[128,4096]{1,0:T(8,128)(2,1)} %bitcast.21, bf16[1024,896]{1,0:T(8,128)(2,1)} %bitcast.19, ...), custom_call_target="tpu_custom_call" | custom-call | flops 22548578304 | bytes 29360128 | tf_op jit(solution)/shard_map/joint/pallas_call | solution.py:587
  101.4 0.0 copy-start
  101.4 2.4 %copy.24 = bf16[1,128,4096]{2,1,0:T(8,128)(2,1)} copy(bf16[1,128,4096]{2,1,0:T(8,128)(2,1)} %bitcast.17) | data formatting | bytes 2097152
  103.8 3.2 %copy.25 = bf16[1,1024,896]{2,1,0:T(8,128)(2,1)} copy(bf16[1,1024,896]{2,1,0:T(8,128)(2,1)} %bitcast.16) | data formatting | bytes 3670016
  107.0 2.9 %copy.26 = bf16[1,1024,896]{2,1,0:T(8,128)(2,1)} copy(bf16[1,1024,896]{2,1,0:T(8,128)(2,1)} %bitcast.15) | data formatting | bytes 3670016
  109.9 0.0 copy-done
  109.9 0.0 slice-start
  109.9 3.7 %copy.27 = bf16[1,896,4096]{2,1,0:T(8,128)(2,1)} copy(bf16[1,896,4096]{2,1,0:T(8,128)(2,1)S(1)} %bitcast.14) | data formatting | bytes 14680064
  113.6 0.0 slice-start.1
  113.6 7.3 %copy.28 = bf16[896,4096]{1,0:T(8,128)(2,1)} copy(bf16[896,4096]{1,0:T(8,128)(2,1)} %get-tuple-element.28) | data formatting | bytes 14680064
  120.9 0.0 slice-done
  120.9 0.0 slice-done.1
  120.9 3.0 %copy.29 = bf16[896,4096]{1,0:T(8,128)(2,1)} copy(bf16[896,4096]{1,0:T(8,128)(2,1)S(1)} %bitcast.13) | data formatting | bytes 14680064
  (1 shorter events, 0.0 us)
Async XLA Ops:
  101.4 8.5 %copy-start = (bf16[896,4096]{1,0:T(8,128)(2,1)S(1)}, bf16[896,4096]{1,0:T(8,128)(2,1)}, u32[]{:S(2)}) copy-start(bf16[896,4096]{1,0:T(8,128)(2,1)} %get-tuple-element.15) | copy-start | bytes 22020100
  109.9 11.0 %slice-start = ((s8[7340032]{0:T(1024)(128)(4,1)}), s8[4194304]{0:T(1024)(128)(4,1)S(1)}, s32[]{:S(2)}) async-start(s8[7340032]{0:T(1024)(128)(4,1)} %bitcast.12), calls=%async_computation | async-start | bytes 8388608
  113.6 7.3 %slice-start.1 = ((s8[7340032]{0:T(1024)(128)(4,1)}), s8[3145728]{0:T(1024)(128)(4,1)S(1)}, s32[]{:S(2)}) async-start(s8[7340032]{0:T(1024)(128)(4,1)} %bitcast.12), calls=%async_computation.1 | async-start | bytes 6291456

commit v2 on v1

--- a/solution.py
+++ b/solution.py
@@ -18,8 +18,10 @@
 LANES = 128
 UNROLL = 4
 MESH = pl.DeviceIdType.MESH
-VMEM_BYTES = 66_000_000
+VMEM_BYTES = 37 * 2**20
+PUT_BYTES = 2**20
 CHUNKS = 4
+FIRST = 2
 
 
 def cosine_table(length):
@@ -151,37 +153,34 @@
     n, replicas,
     residual, gate, up, weight, grads, index, value, right_ref, left_ref,
     output, gate_grad, up_grad, weight_grad, update, updated,
-    dall, slot_up, slot_dn, part, peer, w_v, hidden, hidden_t, gate_v, up_v, res_v,
-    index_v, value_v, row_v, col_v, amount_v, mixed, upd_st, new_st, gg_st, ug_st, wg_st, fin,
+    dall, slot_up, slot_dn, part, w_v, hidden, hidden_t,
+    index_v, value_v, word_v, amount_v, mixed, fin,
     load_sem, comp_send, comp_recv, step_send, step_recv, chip_send, chip_recv,
-    part_send, part_recv, upd_sem, new_sem, gg_sem, ug_sem, wg_sem, out_sem,
+    part_send, part_recv,
 ):
     chips = n // 2
     rep = lax.axis_index("rep")
     me = lax.axis_index("tp")
     z, core = me // 2, me % 2
     partner = me + 1 - 2 * core
-    tokens, units = gate_v.shape
+    tokens, units = gate_grad.shape
     model = w_v.shape[1]
     block = tokens // n
     piece = block // CHUNKS
-    span_rows, listed = index_v.shape[1], index_v.shape[2]
+    span_rows, listed = value_v.shape[1], value_v.shape[2]
     groups = listed // LANES
     per_group = LANES // TOPK
     width = per_group * SPAN
     f32, bf16 = jnp.float32, jnp.bfloat16
 
-    def cond(pred):
-        return pl.when(pred)
-
     loads = [
-        pltpu.make_async_copy(gate, gate_v, load_sem.at[0]),
-        pltpu.make_async_copy(up, up_v, load_sem.at[1]),
+        pltpu.make_async_copy(gate, gate_grad, load_sem.at[0]),
+        pltpu.make_async_copy(up, up_grad, load_sem.at[1]),
         pltpu.make_async_copy(weight, w_v, load_sem.at[2]),
         pltpu.make_async_copy(grads, dall.at[rows_at(me * block, block)], load_sem.at[3]),
         pltpu.make_async_copy(index, index_v.at[rep], load_sem.at[4]),
         pltpu.make_async_copy(value, value_v.at[rep], load_sem.at[5]),
-        pltpu.make_async_copy(residual, res_v, load_sem.at[6]),
+        pltpu.make_async_copy(residual, output, load_sem.at[6]),
     ]
     for load in loads:
         load.start()
@@ -189,11 +188,11 @@
     barrier = pltpu.get_barrier_semaphore()
     has_up, has_dn = z < chips - 1, z > 0
 
-    @cond(has_up)
+    @pl.when(has_up)
     def _():
         pl.semaphore_signal(barrier, inc=1, device_id={"tp": me + 2}, device_id_type=MESH)
 
-    @cond(has_dn)
+    @pl.when(has_dn)
     def _():
         pl.semaphore_signal(barrier, inc=1, device_id={"tp": me - 2}, device_id_type=MESH)
 
@@ -220,10 +219,12 @@
             device_id={"tp": partner}, device_id_type=MESH,
         )
 
+    lent = units - chips * block
+
     def hand_over(target):
         return pltpu.make_async_remote_copy(
-            src_ref=part.at[rows_at((2 * target + 1 - core) * block, block)],
-            dst_ref=peer.at[rows_at(target * block, block)],
+            src_ref=update.at[pl.ds(lent + target * block, block)],
+            dst_ref=weight_grad.at[pl.ds(target * block, block)],
             send_sem=part_send.at[target], recv_sem=part_recv.at[target],
             device_id={"tp": partner}, device_id_type=MESH,
         )
@@ -245,7 +246,7 @@
 
     for q in range(CHUNKS):
         for way in range(2):
-            @cond(onward[way])
+            @pl.when(onward[way])
             def _():
                 send(way, q, grads.at[pl.ds(q * piece, piece)], grad_piece(z, q)).start()
 
@@ -258,9 +259,7 @@
         to_partner(z, q).start()
 
     def own_sum(target, q):
-        mine = part[rows_at((2 * target + core) * block + q * piece, piece), :].astype(f32)
-        other = peer[rows_at(target * block + q * piece, piece), :].astype(f32)
-        return mine + other
+        return part[rows_at(target * block + q * piece, piece), :]
 
     def slot_rows(p, q):
         return rows_at((p - 1) * block + q * piece, piece)
@@ -275,118 +274,135 @@
             summing = jnp.logical_and(jnp.logical_and(p >= at, onward[way]), p < chips - 1)
             first = at == 0
 
-            @cond(behind[way])
+            @pl.when(behind[way])
             def _():
                 send(way, s, grad_piece(z, q), grad_piece(z, q)).wait_recv()
 
-            @cond(gathered)
+            @pl.when(gathered)
             def _():
                 to_partner(source, q).start()
 
-                @cond(onward[way])
+                @pl.when(onward[way])
                 def _():
                     send(way, s + CHUNKS, grad_piece(source, q), grad_piece(source, q)).start()
 
-            @cond(jnp.logical_and(summing, first))
-            def _():
-                slot[slot_rows(p + 1, q), :] = own_sum(target, q).astype(bf16)
-                send(way, s + CHUNKS, slot.at[slot_rows(p + 1, q)], slot.at[slot_rows(p + 1, q)]).start()
-
-            @cond(jnp.logical_and(summing, jnp.logical_not(first)))
+            @pl.when(jnp.logical_and(summing, first))
+            def _():
+                mine = part.at[rows_at(target * block + q * piece, piece)]
+                send(way, s + CHUNKS, mine, slot.at[slot_rows(p + 1, q)]).start()
+
+            @pl.when(jnp.logical_and(summing, jnp.logical_not(first)))
             def _():
                 here = slot_rows(p, q)
-                slot[here, :] = (own_sum(target, q) + slot[here, :].astype(f32)).astype(bf16)
+                slot[here, :] = (own_sum(target, q).astype(f32) + slot[here, :].astype(f32)).astype(bf16)
                 send(way, s + CHUNKS, slot.at[here], slot.at[slot_rows(p + 1, q)]).start()
-
-    def put_output(q):
-        return pltpu.make_async_copy(fin_b.at[pl.ds(q * piece, piece)], output.at[pl.ds(q * piece, piece)], out_sem.at[q])
-
-    fin_b = res_v
 
     def finish(q):
         here = pl.ds(q * piece, piece)
-        fin[...] = res_v[here, :].astype(f32) + own_sum(z, q)
+        fin[...] = output[here, :].astype(f32) + own_sum(z, q).astype(f32)
         for way in range(2):
-            @cond(behind[way])
+            @pl.when(behind[way])
             def _():
                 fin[...] = fin[...] + slots[way][pl.ds((chips - 2) * block + q * piece, piece), :].astype(f32)
-        res_v[here, :] = fin[...].astype(bf16)
-        put_output(q).start()
+        output[here, :] = fin[...].astype(bf16)
 
     loads[0].wait()
     loads[1].wait()
 
     def make_hidden(i, carry):
-        here = rows_at(i * LANES, LANES)
-        g = gate_v[here, :].astype(f32)
-        u = up_v[here, :].astype(f32)
+        here = rows_at(i * block, block)
+        g = gate_grad[here, :].astype(f32)
+        u = up_grad[here, :].astype(f32)
         h = (g * jax.nn.sigmoid(g) * u).astype(bf16)
         hidden[here, :] = h
         hidden_t[:, here] = h.astype(f32).T.astype(bf16)
         return carry
 
-    lax.fori_loop(0, tokens // LANES, make_hidden, 0)
+    tile = 512
+
+    def target_at(k):
+        return jnp.where(k % 2 == 0, chips - 1 - k // 2, k // 2)
+
+    def add_other(k):
+        target = target_at(k)
+        hand_over(target).wait_recv()
+
+        def add_part(q, carry):
+            here = rows_at(target * block + q * piece, piece)
+            part[here, :] = (part[here, :].astype(f32) + weight_grad[here, :].astype(f32)).astype(bf16)
+            return carry
+
+        lax.fori_loop(0, CHUNKS, add_part, 0)
+
+    def make_target(k, carry):
+        target = target_at(k)
+        lax.fori_loop(2 * target, 2 * target + 2, make_hidden, 0)
+        rows = rows_at(2 * target * block, 2 * block)
+        mine, other = rows_at(target * block, block), rows_at(lent + target * block, block)
+
+        def make_part(i, carry):
+            here = rows_at(i * tile, tile)
+            got = jnp.dot(hidden[rows, :], w_v[:, here], preferred_element_type=f32).astype(bf16)
+
+            @pl.when(core == 0)
+            def _():
+                part[mine, here] = got[:block]
+                update[other, here] = got[block:]
+
+            @pl.when(core == 1)
+            def _():
+                part[mine, here] = got[block:]
+                update[other, here] = got[:block]
+            return carry
+
+        lax.fori_loop(0, model // tile, make_part, 0)
+        hand_over(target).start()
+
+        @pl.when(k > 0)
+        def _():
+            add_other(k - 1)
+
+        @pl.when(k >= FIRST)
+        def _():
+            service(k - FIRST)
+
+        return carry
 
     loads[2].wait()
-    tile = 512
-
-    def make_part(i, carry):
-        here = rows_at(i * tile, tile)
-        part[:, here] = jnp.dot(hidden[...], w_v[:, here], preferred_element_type=f32).astype(bf16)
-        return carry
-
-    lax.fori_loop(0, model // tile, make_part, 0)
-    order = []
-    for k in range(chips):
-        order.append(chips - 1 - k // 2 if k % 2 == 0 else k // 2)
-    for target in order:
-        hand_over(target).start()
+    lax.fori_loop(0, chips, make_target, 0)
 
     for step in range(1, replicas):
         for copy in comp_copies(step):
             copy.wait_recv()
     loads[4].wait()
     loads[5].wait()
+
     pairs = replicas // 2
     half = LANES // 2
-    spot = lax.broadcasted_iota(jnp.int32, (span_rows, listed), 1)
+    spot = lax.broadcasted_iota(jnp.int32, (1, listed), 1)
     lower = spot % LANES < half
-    shift = ((spot // TOPK) % 2) * SPAN
-
-    def spread_out(dest, arrays):
+    for a in range(span_rows):
         for j in range(pairs):
-            even, odd = arrays[2 * j], arrays[2 * j + 1]
-            first = jnp.where(lower, even, pltpu.roll(odd, half, 1))
-            second = jnp.where(lower, pltpu.roll(even, listed - half, 1), odd)
-            for a in range(span_rows):
-                dest[a, j:j + 1, :] = first[a:a + 1]
-                dest[a, pairs + j:pairs + j + 1, :] = second[a:a + 1]
-
-    spread_out(row_v, [(index_v[r] >> (SPAN.bit_length() - 1)).astype(f32) for r in range(replicas)])
-    spread_out(col_v, [((index_v[r] & (SPAN - 1)) + shift).astype(f32) for r in range(replicas)])
-    spread_out(amount_v, [value_v[r].astype(f32) for r in range(replicas)])
+            for dest, pick in (
+                (word_v, lambda r: index_v[r, a]),
+                (amount_v, lambda r: value_v[r].astype(f32)[a:a + 1]),
+            ):
+                even, odd = pick(2 * j), pick(2 * j + 1)
+                dest[a, j:j + 1, :] = jnp.where(lower, even, pltpu.roll(odd, half, 1))
+                dest[a, pairs + j:pairs + j + 1, :] = jnp.where(lower, pltpu.roll(even, listed - half, 1), odd)
+
     deep = pairs * LANES
+    shift = ((lax.broadcasted_iota(jnp.int32, (replicas, LANES), 1) // TOPK) % 2) * SPAN
     row_place = lax.broadcasted_iota(jnp.int32, (SPAN, deep), 0).astype(f32).astype(bf16)
     col_place = lax.broadcasted_iota(jnp.int32, (2 * SPAN, deep), 0).astype(f32).astype(bf16)
 
-    def put_update(a, k):
-        rows = rows_at(a * SPAN, SPAN)
-        return (
-            pltpu.make_async_copy(upd_st.at[k], update.at[rows], upd_sem.at[k]),
-            pltpu.make_async_copy(new_st.at[k], updated.at[rows], new_sem.at[k]),
-        )
-
     def decode_row(a):
-        k = a % 2
-
-        @cond(a >= 2)
-        def _():
-            for copy in put_update(a, k):
-                copy.wait()
-
         def gather(group, carry):
             at = rows_at(group * LANES, LANES)
-            row_set, col_set, amount_set = row_v[a, :, at], col_v[a, :, at], amount_v[a, :, at]
+            words = word_v[a, :, at]
+            row_set = (words >> (SPAN.bit_length() - 1)).astype(f32)
+            col_set = ((words & (SPAN - 1)) + shift).astype(f32)
+            amount_set = amount_v[a, :, at]
             for side in range(2):
                 line = lambda x: jnp.concatenate(
                     [x[side * pairs + j:side * pairs + j + 1] for j in range(pairs)], axis=1
@@ -401,43 +417,30 @@
 
         lax.fori_loop(0, groups, gather, 0, unroll=UNROLL)
         halfway = jnp.dot(mixed[...], right_ref[...], preferred_element_type=f32).astype(bf16)
+        rows = rows_at(a * SPAN, SPAN)
         for group in range(groups):
             spread = jnp.dot(
                 left_ref[...], halfway[group * SPAN:(group + 1) * SPAN], preferred_element_type=f32
             )
             change = (spread * (1.0 / replicas)).astype(bf16)
             at = slice(group * width, (group + 1) * width)
-            upd_st[k, :, at] = change
-            new_st[k, :, at] = (
-                w_v[rows_at(a * SPAN, SPAN), at].astype(f32) - learn_rate * change.astype(f32)
-            ).astype(bf16)
-        for copy in put_update(a, k):
-            copy.start()
-
-    early = CHUNKS - 1
-    decode_head = 2
+            update[rows, at] = change
+            updated[rows, at] = (w_v[rows, at].astype(f32) - learn_rate * change.astype(f32)).astype(bf16)
 
     def decode_step(a, carry):
         decode_row(a)
 
-        @cond(a == decode_head - 1)
+        @pl.when(a % 2 == 1)
         def _():
-            for target in order:
-                hand_over(target).wait_recv()
-            for s in range(early):
-                service(s)
-
-        @cond(jnp.logical_and(a >= decode_head, a % 2 == 1))
-        def _():
-            service(early + (a - decode_head) // 2)
+            service(chips - FIRST + a // 2)
 
         return carry
 
+    add_other(chips - 1)
+    for target in range(chips):
+        hand_over(target).wait_send()
     lax.fori_loop(0, span_rows, decode_step, 0)
-    served = early + (span_rows - decode_head) // 2
-    for k in range(2):
-        for copy in put_update(span_rows - 2 + k, k):
-            copy.wait()
+    served = chips - FIRST + span_rows // 2
 
     def serve_to(start, stop):
         if stop > start:
@@ -445,69 +448,37 @@
 
     low = z < chips // 2
 
-    def put_grads(start, k):
-        rows = rows_at(start, 2 * block)
-        return (
-            pltpu.make_async_copy(gg_st.at[k], gate_grad.at[rows], gg_sem.at[k]),
-            pltpu.make_async_copy(ug_st.at[k], up_grad.at[rows], ug_sem.at[k]),
-        )
-
-    def wait_chip(chip):
+    def grads_of(k, carry):
+        chip = jnp.where(low, k, chips - 1 - k)
         for q in range(CHUNKS):
             to_partner(chip, q).wait_recv()
-
-    def chip_at(k):
-        return jnp.where(low, k, chips - 1 - k)
-
-    def grads_of(k, carry):
-        chip = chip_at(k)
-        start = chip * 2 * block
-        wait_chip(chip)
-        j = k % 2
-
-        @cond(k >= 2)
-        def _():
-            for copy in put_grads(start, j):
-                copy.wait()
-
-        rows = rows_at(start, 2 * block)
+        rows = rows_at(chip * 2 * block, 2 * block)
         back = lax.dot_general(
             dall[rows, :], w_v[...], (((1,), (1,)), ((), ())), preferred_element_type=f32
         )
-        g = gate_v[rows, :].astype(f32)
-        u = up_v[rows, :].astype(f32)
+        g = gate_grad[rows, :].astype(f32)
+        u = up_grad[rows, :].astype(f32)
         sig = jax.nn.sigmoid(g)
-        gg_st[j] = (back * u * sig * (1.0 + g * (1.0 - sig))).astype(bf16)
-        ug_st[j] = (back * (g * sig)).astype(bf16)
-        for copy in put_grads(start, j):
-            copy.start()
+        gate_grad[rows, :] = (back * u * sig * (1.0 + g * (1.0 - sig))).astype(bf16)
+        up_grad[rows, :] = (back * (g * sig)).astype(bf16)
         return carry
 
-    serve_to(served, 2 * CHUNKS + 1)
+    serve_to(served, 2 * CHUNKS)
     lax.fori_loop(0, chips // 2, grads_of, 0)
-    serve_to(2 * CHUNKS + 1, (chips - 1) * CHUNKS)
+    serve_to(max(served, 2 * CHUNKS), (chips - 1) * CHUNKS)
     lax.fori_loop(chips // 2, chips, grads_of, 0)
 
     wide = 256
     last = (chips - 1) * CHUNKS
+    loads[6].wait()
     service(last)
-    loads[6].wait()
     finish(0)
 
-    def put_weight(i, k):
-        return pltpu.make_async_copy(wg_st.at[k], weight_grad.at[:, rows_at(i * wide, wide)], wg_sem.at[k])
-
     def make_weight(i, carry):
-        k = i % 2
-
-        @cond(i >= 2)
-        def _():
-            put_weight(i, k).wait()
-
-        wg_st[k] = jnp.dot(
-            hidden_t[...], dall[:, rows_at(i * wide, wide)], preferred_element_type=f32
+        here = rows_at(i * wide, wide)
+        weight_grad[:, here] = jnp.dot(
+            hidden_t[...], dall[:, here], preferred_element_type=f32
         ).astype(bf16)
-        put_weight(i, k).start()
         return carry
 
     turns = model // wide
@@ -517,14 +488,6 @@
         service(last + q)
         finish(q)
 
-    for k in range(2):
-        put_weight(turns - 2 + k, k).wait()
-        for copy in put_grads(0, k):
-            copy.wait()
-    for q in range(CHUNKS):
-        put_output(q).wait()
-    for target in range(chips):
-        hand_over(target).wait_send()
     for chip in range(chips):
         for q in range(CHUNKS):
             to_partner(chip, q).wait_send()
@@ -532,7 +495,7 @@
         for copy in comp_copies(step):
             copy.wait_send()
     for way in range(2):
-        @cond(onward[way])
+        @pl.when(onward[way])
         def _():
             for s in range(chips * CHUNKS):
                 send(way, s, grad_piece(z, 0), grad_piece(z, 0)).wait_send()
@@ -546,25 +509,15 @@
         ((tokens, model), bf16),
         (((chips - 1) * block, model), bf16),
         (((chips - 1) * block, model), bf16),
-        ((tokens, model), bf16),
         ((chips * block, model), bf16),
         ((units, model), bf16),
         ((tokens, units), bf16),
         ((units, tokens), bf16),
-        ((tokens, units), bf16),
-        ((tokens, units), bf16),
-        ((block, model), bf16),
-        ((replicas, span_rows, listed), jnp.int32),
+        ((replicas, span_rows, 1, listed), jnp.int32),
         ((replicas, span_rows, listed), bf16),
-        ((span_rows, replicas, listed), f32),
-        ((span_rows, replicas, listed), f32),
+        ((span_rows, replicas, listed), jnp.int32),
         ((span_rows, replicas, listed), f32),
         ((listed // LANES * SPAN, LANES // TOPK * SPAN), bf16),
-        ((2, SPAN, model), bf16),
-        ((2, SPAN, model), bf16),
-        ((2, 2 * block, units), bf16),
-        ((2, 2 * block, units), bf16),
-        ((2, units, 256), bf16),
         ((block // CHUNKS, model), f32),
     ]
     total = sum(int(np.prod(shape)) * jnp.dtype(kind).itemsize for shape, kind in arrays)
@@ -572,7 +525,6 @@
     sems = [
         dma((7,)), dma((2, replicas - 1)), dma((2, replicas - 1)), dma((2, steps)), dma((2, steps)),
         dma((steps,)), dma((steps,)), dma((chips,)), dma((chips,)),
-        dma((2,)), dma((2,)), dma((2,)), dma((2,)), dma((2,)), dma((CHUNKS,)),
     ]
     return total, [pltpu.VMEM(shape, kind) for shape, kind in arrays] + sems
 
@@ -583,15 +535,12 @@
     right, left = decode_tables()
     any_spec = pl.BlockSpec(memory_space=pl.ANY)
     vmem_spec = pl.BlockSpec(memory_space=pltpu.VMEM)
-    shape = lambda *dims: jax.ShapeDtypeStruct(dims, jnp.bfloat16)
-    return pl.pallas_call(
+    shapes = [residual_r.shape, (tokens, units), (tokens, units)] + [(units, model)] * 3
+    kept = pl.pallas_call(
         functools.partial(joint_kernel, n, replicas),
-        out_shape=[
-            shape(*residual_r.shape), shape(tokens, units), shape(tokens, units),
-            shape(units, model), shape(units, model), shape(units, model),
-        ],
+        out_shape=[pltpu.VMEM(shape, jnp.bfloat16) for shape in shapes],
         in_specs=[any_spec] * 7 + [vmem_spec] * 2,
-        out_specs=[any_spec] * 6,
+        out_specs=[vmem_spec] * 6,
         scratch_shapes=scratch,
         compiler_params=pltpu.CompilerParams(
             collective_id=0, has_side_effects=True, vmem_limit_bytes=VMEM_BYTES
@@ -600,7 +549,29 @@
             flops=6 * tokens * units * model, bytes_accessed=units * model * 8, transcendentals=0
         ),
         name="joint",
-    )(residual_r, gate_r, up_r, down_weight, grads_r, index_r, value_r, right, left)
+    )(residual_r, gate_r, up_r, down_weight, grads_r, index_r[:, None], value_r, right, left)
+    return pl.pallas_call(
+        put_kernel,
+        out_shape=[jax.ShapeDtypeStruct(shape, jnp.bfloat16) for shape in shapes],
+        in_specs=[vmem_spec] * 6,
+        out_specs=[any_spec] * 6,
+        scratch_shapes=[pltpu.SemaphoreType.DMA((6,))],
+        compiler_params=pltpu.CompilerParams(vmem_limit_bytes=PUT_BYTES),
+        name="put",
+    )(*kept)
+
+
+def put_kernel(*refs):
+    sem = refs[-1]
+    copies = [pltpu.make_async_copy(refs[i], refs[6 + i], sem.at[i]) for i in range(6)]
+    for copy in copies:
+        copy.start()
+    for copy in copies:
+        copy.wait()
+
+
+def chips_rows(n, tokens):
+    return n // 2 * (tokens // n)
 
 
 def shards(residual, gate_pre, up_pre, down_weight, d_out, comp_index, comp_value):
@@ -612,7 +583,7 @@
     fits = False
     if n % 4 == 0 and units % LANES == 0 and span_rows % 2 == 0 and replicas % 2 == 0:
         total, scratch = joint_scratch(n, replicas, tokens, units, model, span_rows, listed)
-        fits = total < 56 * 2**20 and n // 2 == CHUNKS
+        fits = total < 36 * 2**20 and units >= chips_rows(n, tokens) and n // 2 == CHUNKS
     if fits:
         outs = joint(*operands, scratch)
     else:

time: 124 us -> 108 us (0.87)
  local copies, waits for them, and re-layouts: 24.2 us -> 0 us
  Pallas kernels: 99.1 us -> 107 us
    unnamed x13 -> x0, local copies, waits for them, and re-layouts: 24.2 us -> none
    pallas_call x1 -> x2, Pallas kernels: 99.1 us -> 107 us  [the longest x1 98.3 us: joint(): pl.pallas_call(functools.partial(joint_kernel, n, replicas), out_shape=[p...]
where the time goes in v2:
time: 108 us
  Pallas kernels  107 us (99%)
    pallas_call x1, Pallas kernels, joint(): pl.pallas_call(functools.partial(joint_kernel, n, replicas), out_shape=[p...  98.3 us
    pallas_call x1, Pallas kernels, joint(): pl.pallas_call(put_kernel, out_shape=[jax.ShapeDtypeStruct(shape, jnp.bfl...  9.07 us

profile of v2, /device:TPU:0, one launch (start us, length us, event | category | flops | bytes accessed | tf_op | source)
XLA Modules:
  0.0 108.0 jit_solution(1444902480969669399)
XLA Ops:
  0.6 98.3 %joint.1 = (bf16[128,4096]{1,0:T(8,128)(2,1)S(1)}, bf16[1024,896]{1,0:T(8,128)(2,1)S(1)}, bf16[1024,896]{1,0:T(8,128)(2,1)S(1)}, bf16[896,4096]{1,0:T(8,128)(2,1...) custom-call(bf16[128,4096]{1,0:T(8,128)(2,1)} %bitcast.15, bf16[1024,896]{1,0:T(8,128)(2,1)} %bitcast.11, ...), custom_call_target="tpu_custom_call" | custom-call | flops 22548578304 | bytes 29360128 | tf_op jit(solution)/shard_map/joint/pallas_call | solution.py:539
  98.9 9.1 %put.1 = (bf16[128,4096]{1,0:T(8,128)(2,1)}, bf16[1024,896]{1,0:T(8,128)(2,1)}, bf16[1024,896]{1,0:T(8,128)(2,1)}, bf16[896,4096]{1,0:T(8,128)(2,1)}, bf16[896,4...) custom-call(bf16[128,4096]{1,0:T(8,128)(2,1)S(1)} %get-tuple-element.18.refs_0_, ...), custom_call_target="tpu_custom_call" | custom-call | tf_op jit(solution)/shard_map/put/pallas_call | solution.py:553

commit v3 on v2

--- a/solution.py
+++ b/solution.py
@@ -18,7 +18,7 @@
 LANES = 128
 UNROLL = 4
 MESH = pl.DeviceIdType.MESH
-VMEM_BYTES = 37 * 2**20
+VMEM_BYTES = 38 * 2**20
 PUT_BYTES = 2**20
 CHUNKS = 4
 FIRST = 2
@@ -152,11 +152,11 @@
 def joint_kernel(
     n, replicas,
     residual, gate, up, weight, grads, index, value, right_ref, left_ref,
-    output, gate_grad, up_grad, weight_grad, update, updated,
+    output, gate_grad, up_grad, weight_grad, update, updated, late,
     dall, slot_up, slot_dn, part, w_v, hidden, hidden_t,
     index_v, value_v, word_v, amount_v, mixed, fin,
     load_sem, comp_send, comp_recv, step_send, step_recv, chip_send, chip_recv,
-    part_send, part_recv,
+    part_send, part_recv, late_sem,
 ):
     chips = n // 2
     rep = lax.axis_index("rep")
@@ -264,6 +264,9 @@
     def slot_rows(p, q):
         return rows_at((p - 1) * block + q * piece, piece)
 
+    def put_late(source, q):
+        return pltpu.make_async_copy(source, late.at[rows_at(q * piece, piece)], late_sem.at[q])
+
     def service(s):
         p, q = s // CHUNKS, s % CHUNKS
         for way in range(2):
@@ -274,7 +277,18 @@
             summing = jnp.logical_and(jnp.logical_and(p >= at, onward[way]), p < chips - 1)
             first = at == 0
 
-            @pl.when(behind[way])
+            def pass_on(source):
+                after = jnp.logical_and(p == chips - 2, core == way)
+
+                @pl.when(after)
+                def _():
+                    put_late(source, q).start()
+
+                @pl.when(jnp.logical_not(after))
+                def _():
+                    send(way, s + CHUNKS, source, slot.at[slot_rows(p + 1, q)]).start()
+
+            @pl.when(jnp.logical_and(behind[way], jnp.logical_or(p < chips - 1, core != way)))
             def _():
                 send(way, s, grad_piece(z, q), grad_piece(z, q)).wait_recv()
 
@@ -288,22 +302,21 @@
 
             @pl.when(jnp.logical_and(summing, first))
             def _():
-                mine = part.at[rows_at(target * block + q * piece, piece)]
-                send(way, s + CHUNKS, mine, slot.at[slot_rows(p + 1, q)]).start()
+                pass_on(part.at[rows_at(target * block + q * piece, piece)])
 
             @pl.when(jnp.logical_and(summing, jnp.logical_not(first)))
             def _():
                 here = slot_rows(p, q)
                 slot[here, :] = (own_sum(target, q).astype(f32) + slot[here, :].astype(f32)).astype(bf16)
-                send(way, s + CHUNKS, slot.at[here], slot.at[slot_rows(p + 1, q)]).start()
+                pass_on(slot.at[here])
 
     def finish(q):
-        here = pl.ds(q * piece, piece)
+        here = rows_at(q * piece, piece)
         fin[...] = output[here, :].astype(f32) + own_sum(z, q).astype(f32)
         for way in range(2):
-            @pl.when(behind[way])
-            def _():
-                fin[...] = fin[...] + slots[way][pl.ds((chips - 2) * block + q * piece, piece), :].astype(f32)
+            @pl.when(jnp.logical_and(behind[way], core != way))
+            def _():
+                fin[...] = fin[...] + slots[way][rows_at((chips - 2) * block + q * piece, piece), :].astype(f32)
         output[here, :] = fin[...].astype(bf16)
 
     loads[0].wait()
@@ -430,9 +443,9 @@
     def decode_step(a, carry):
         decode_row(a)
 
-        @pl.when(a % 2 == 1)
+        @pl.when(a % 3 == 2)
         def _():
-            service(chips - FIRST + a // 2)
+            service(chips - FIRST + a // 3)
 
         return carry
 
@@ -440,11 +453,7 @@
     for target in range(chips):
         hand_over(target).wait_send()
     lax.fori_loop(0, span_rows, decode_step, 0)
-    served = chips - FIRST + span_rows // 2
-
-    def serve_to(start, stop):
-        if stop > start:
-            lax.fori_loop(start, stop, lambda s, carry: (service(s), carry)[1], 0)
+    served = chips - FIRST + span_rows // 3
 
     low = z < chips // 2
 
@@ -463,30 +472,60 @@
         up_grad[rows, :] = (back * (g * sig)).astype(bf16)
         return carry
 
-    serve_to(served, 2 * CHUNKS)
-    lax.fori_loop(0, chips // 2, grads_of, 0)
-    serve_to(max(served, 2 * CHUNKS), (chips - 1) * CHUNKS)
-    lax.fori_loop(chips // 2, chips, grads_of, 0)
+    def serve_loop(start, stop):
+        lax.fori_loop(start, stop, lambda s, carry: (service(s), carry)[1], 0)
+
+    def grads_early(k, carry):
+        grads_of(k, carry)
+
+        @pl.when(served + k < 2 * CHUNKS)
+        def _():
+            service(served + k)
+
+        return carry
 
     wide = 256
+    turns = model // wide
     last = (chips - 1) * CHUNKS
+    near = 2 * block * (chips - 1)
+    near_at = jnp.where(low, 0, 2 * block)
+    far_at = jnp.where(low, near, 0)
+    between = CHUNKS - 1
+
+    def weight_near(i, carry):
+        here = rows_at(i * wide, wide)
+        rows = pl.ds(pl.multiple_of(near_at, 2 * block), near)
+        weight_grad[:, here] = jnp.dot(
+            hidden_t[:, rows], dall[rows, here], preferred_element_type=f32
+        ).astype(bf16)
+
+        @pl.when(i % (turns // between) == turns // between - 1)
+        def _():
+            service(2 * CHUNKS + i // (turns // between))
+
+        return carry
+
+    def weight_far(i, carry):
+        here = rows_at(i * wide, wide)
+        rows = rows_at(far_at, 2 * block)
+        more = jnp.dot(hidden_t[:, rows], dall[rows, here], preferred_element_type=f32)
+        weight_grad[:, here] = (weight_grad[:, here].astype(f32) + more).astype(bf16)
+
+        @pl.when(i % (turns // CHUNKS) == turns // CHUNKS - 1)
+        def _():
+            service(last + i // (turns // CHUNKS))
+            finish(i // (turns // CHUNKS))
+
+        return carry
+
+    lax.fori_loop(0, chips - 2, grads_early, 0)
+    serve_loop(served + chips - 2, 2 * CHUNKS)
+    grads_of(chips - 2, 0)
+    lax.fori_loop(0, turns, weight_near, 0)
+    service(last - 1)
+    grads_of(chips - 1, 0)
     loads[6].wait()
-    service(last)
-    finish(0)
-
-    def make_weight(i, carry):
-        here = rows_at(i * wide, wide)
-        weight_grad[:, here] = jnp.dot(
-            hidden_t[...], dall[:, here], preferred_element_type=f32
-        ).astype(bf16)
-        return carry
-
-    turns = model // wide
-    marks = [turns * k // (CHUNKS - 1) for k in range(CHUNKS)]
-    for q in range(1, CHUNKS):
-        lax.fori_loop(marks[q - 1], marks[q], make_weight, 0)
-        service(last + q)
-        finish(q)
+    lax.fori_loop(0, turns, weight_far, 0)
 
     for chip in range(chips):
         for q in range(CHUNKS):
@@ -497,8 +536,18 @@
     for way in range(2):
         @pl.when(onward[way])
         def _():
-            for s in range(chips * CHUNKS):
+            for s in range(last):
                 send(way, s, grad_piece(z, 0), grad_piece(z, 0)).wait_send()
+
+            @pl.when(core != way)
+            def _():
+                for s in range(last, last + CHUNKS):
+                    send(way, s, grad_piece(z, 0), grad_piece(z, 0)).wait_send()
+
+            @pl.when(core == way)
+            def _():
+                for q in range(CHUNKS):
+                    put_late(part.at[pl.ds(0, piece)], q).wait()
 
 
 def joint_scratch(n, replicas, tokens, units, model, span_rows, listed):
@@ -524,7 +573,7 @@
     steps = chips * CHUNKS
     sems = [
         dma((7,)), dma((2, replicas - 1)), dma((2, replicas - 1)), dma((2, steps)), dma((2, steps)),
-        dma((steps,)), dma((steps,)), dma((chips,)), dma((chips,)),
+        dma((steps,)), dma((steps,)), dma((chips,)), dma((chips,)), dma((CHUNKS,)),
     ]
     return total, [pltpu.VMEM(shape, kind) for shape, kind in arrays] + sems
 
@@ -536,11 +585,12 @@
     any_spec = pl.BlockSpec(memory_space=pl.ANY)
     vmem_spec = pl.BlockSpec(memory_space=pltpu.VMEM)
     shapes = [residual_r.shape, (tokens, units), (tokens, units)] + [(units, model)] * 3
-    kept = pl.pallas_call(
+    *kept, late = pl.pallas_call(
         functools.partial(joint_kernel, n, replicas),
-        out_shape=[pltpu.VMEM(shape, jnp.bfloat16) for shape in shapes],
+        out_shape=[pltpu.VMEM(shape, jnp.bfloat16) for shape in shapes]
+        + [jax.ShapeDtypeStruct(residual_r.shape, jnp.bfloat16)],
         in_specs=[any_spec] * 7 + [vmem_spec] * 2,
-        out_specs=[vmem_spec] * 6,
+        out_specs=[vmem_spec] * 6 + [any_spec],
         scratch_shapes=scratch,
         compiler_params=pltpu.CompilerParams(
             collective_id=0, has_side_effects=True, vmem_limit_bytes=VMEM_BYTES
@@ -550,20 +600,29 @@
         ),
         name="joint",
     )(residual_r, gate_r, up_r, down_weight, grads_r, index_r[:, None], value_r, right, left)
-    return pl.pallas_call(
+    hops = [(i, i + 2) for i in range(0, n - 2, 2)] + [(i, i - 2) for i in range(3, n, 2)]
+    arrived = lax.ppermute(late, "tp", hops)
+    early, *kept = kept
+    placed = pl.pallas_call(
         put_kernel,
-        out_shape=[jax.ShapeDtypeStruct(shape, jnp.bfloat16) for shape in shapes],
-        in_specs=[vmem_spec] * 6,
-        out_specs=[any_spec] * 6,
-        scratch_shapes=[pltpu.SemaphoreType.DMA((6,))],
+        out_shape=[jax.ShapeDtypeStruct(shape, jnp.bfloat16) for shape in shapes[1:]],
+        in_specs=[vmem_spec] * 5,
+        out_specs=[any_spec] * 5,
+        scratch_shapes=[pltpu.SemaphoreType.DMA((5,))],
         compiler_params=pltpu.CompilerParams(vmem_limit_bytes=PUT_BYTES),
+        cost_estimate=pl.CostEstimate(
+            flops=2 * tokens * units * model, bytes_accessed=units * model * 8, transcendentals=0
+        ),
         name="put",
     )(*kept)
+    output = (early.astype(jnp.float32) + arrived.astype(jnp.float32)).astype(jnp.bfloat16)
+    return [output] + list(placed)
 
 
 def put_kernel(*refs):
     sem = refs[-1]
-    copies = [pltpu.make_async_copy(refs[i], refs[6 + i], sem.at[i]) for i in range(6)]
+    count = len(refs) // 2
+    copies = [pltpu.make_async_copy(refs[i], refs[count + i], sem.at[i]) for i in range(count)]
     for copy in copies:
         copy.start()
     for copy in copies:
@@ -583,7 +642,7 @@
     fits = False
     if n % 4 == 0 and units % LANES == 0 and span_rows % 2 == 0 and replicas % 2 == 0:
         total, scratch = joint_scratch(n, replicas, tokens, units, model, span_rows, listed)
-        fits = total < 36 * 2**20 and units >= chips_rows(n, tokens) and n // 2 == CHUNKS
+        fits = total < 36 * 2**20 and units >= chips_rows(n, tokens) and n // 2 == CHUNKS and 2 * CHUNKS >= CHUNKS - FIRST + span_rows // 3 + 2
     if fits:
         outs = joint(*operands, scratch)
     else:

time: 108 us -> 105 us (0.972)
  Pallas kernels: 107 us -> 96 us
  waiting for transfers between devices: 0 us -> 3.62 us
  starting transfers between devices: 0 us -> 3.55 us
  other arithmetic: 0 us -> 1.22 us
    pallas_call x1, Pallas kernels: 98.3 us -> 87.1 us  [joint(): pl.pallas_call(functools.partial(joint_kernel, n, replicas), out_shape=[p...]
    ppermute x0 -> x1, waiting for transfers between devices: none -> 3.62 us  [joint(): arrived = lax.ppermute(late, 'tp', hops)]
    ppermute x0 -> x1, starting transfers between devices: none -> 3.55 us  [joint(): arrived = lax.ppermute(late, 'tp', hops)]
    broadcast_in_dim x0 -> x1, other arithmetic: none -> 1.22 us  [shards(): output[None]]
  transfers between devices with their start and end apart: 0 -> 1, of which waited for: 0 -> 1; matrix products, arithmetic and copies ran while one was open for 0% -> 0% of each run, Pallas kernels for 0% -> 8%
where the time goes in v3:
time: 105 us
  Pallas kernels  96 us (91%)
  waiting for transfers between devices  3.62 us (3%)
  starting transfers between devices  3.55 us (3%)
  other arithmetic  1.22 us (1%)
    pallas_call x1, Pallas kernels, joint(): pl.pallas_call(functools.partial(joint_kernel, n, replicas), out_shape=[p...  87.1 us
    pallas_call x1, Pallas kernels, joint(): pl.pallas_call(put_kernel, out_shape=[jax.ShapeDtypeStruct(shape, jnp.bfl...  8.92 us
    ppermute x1, waiting for transfers between devices, joint(): arrived = lax.ppermute(late, 'tp', hops)  3.62 us
    ppermute x1, starting transfers between devices, joint(): arrived = lax.ppermute(late, 'tp', hops)  3.55 us
  transfers between devices with their start and end apart: 1, of which 1 were waited for; matrix products, arithmetic and copies ran while one was open for 0% of the time, Pallas kernels for 8%

profile of v3, /device:TPU:0, one launch (start us, length us, event | category | flops | bytes accessed | tf_op | source)
XLA Modules:
  0.0 105.0 jit_solution(12424108957515519531)
XLA Ops:
  0.6 87.1 %joint.1 = (bf16[128,4096]{1,0:T(8,128)(2,1)S(1)}, bf16[1024,896]{1,0:T(8,128)(2,1)S(1)}, bf16[1024,896]{1,0:T(8,128)(2,1)S(1)}, bf16[896,4096]{1,0:T(8,128)(2,1...) custom-call(bf16[128,4096]{1,0:T(8,128)(2,1)} %bitcast.13, ...), custom_call_target="tpu_custom_call" | custom-call | flops 22548578304 | bytes 29360128 | tf_op jit(solution)/shard_map/joint/pallas_call | solution.py:588
  87.7 3.6 %collective-permute-start = (bf16[128,4096]{1,0:T(8,128)(2,1)}, bf16[128,4096]{1,0:T(8,128)(2,1)S(1)}, u32[]{:S(2)}, u32[]{:S(2)}) collective-permute-start(bf16[128,4096]{1,0:T(8,128)(2,1)} %get-tuple-element.19), channel_id=1, source_target_pairs={{0,2},{2,4},{4,6},{3,1},{5,3},{7,5},{8,10},{10,12},{12,14},{11,9},... | collective-permute-start | bytes 3145736 | tf_op jit(solution)/shard_map/ppermute | solution.py:604
  91.3 8.9 %put.1 = (bf16[1024,896]{1,0:T(8,128)(2,1)}, bf16[1024,896]{1,0:T(8,128)(2,1)}, bf16[896,4096]{1,0:T(8,128)(2,1)}, bf16[896,4096]{1,0:T(8,128)(2,1)}, bf16[896,4096]{1,0:T(8,128)(2,1)}) custom-call(bf16[1024,896]{1,0:T(8,128)(2,1)S(1)} %get-tuple-element.20.refs_0_, bf16[1024,896]{1,0:T(8,128)(2,1)S(1)} %get-tuple-element.21.refs_1_, ...), custom_call_target="tpu_custom_call" | custom-call | flops 7516192768 | bytes 29360128 | tf_op jit(solution)/shard_map/put/pallas_call | solution.py:606
  100.2 3.6 %collective-permute-done = bf16[128,4096]{1,0:T(8,128)(2,1)S(1)} collective-permute-done((bf16[128,4096]{1,0:T(8,128)(2,1)}, bf16[128,4096]{1,0:T(8,128)(2,1)S(1)}, u32[]{:S(2)}, u32[]{:S(2)}) %collective-permute-start) | collective-permute-done | bytes 1048608 | tf_op jit(solution)/shard_map/ppermute | solution.py:604
  103.8 1.2 %fusion = bf16[1,128,4096]{2,1,0:T(8,128)(2,1)} fusion(bf16[128,4096]{1,0:T(8,128)(2,1)S(1)} %collective-permute-done, bf16[128,4096]{1,0:T(8,128)(2,1)S(1)} %get-tuple-element.18), kind=kLoop, calls=%fused_computation.1 | loop fusion | flops 2097152 | bytes 3145728 | tf_op jit(solution)/shard_map/broadcast_in_dim | solution.py:652
Async XLA Ops:
  87.7 16.1 %collective-permute-start = (bf16[128,4096]{1,0:T(8,128)(2,1)}, bf16[128,4096]{1,0:T(8,128)(2,1)S(1)}, u32[]{:S(2)}, u32[]{:S(2)}) collective-permute-start(bf16[128,4096]{1,0:T(8,128)(2,1)} %get-tuple-element.19), channel_id=1, source_target_pairs={{0,2},{2,4},{4,6},{3,1},{5,3},{7,5},{8,10},{10,12},{12,14},{11,9},... | collective-permute-start | bytes 3145736 | tf_op jit(solution)/shard_map/ppermute | solution.py:604

commit v4 on v3

--- a/solution.py
+++ b/solution.py
@@ -20,6 +20,7 @@
 MESH = pl.DeviceIdType.MESH
 VMEM_BYTES = 38 * 2**20
 PUT_BYTES = 2**20
+PUT_PARTS = 4
 CHUNKS = 4
 FIRST = 2
 
@@ -149,12 +150,19 @@
     return pl.ds(pl.multiple_of(start, size), size)
 
 
+def flip(place, bits):
+    for k in range(bits.bit_length()):
+        if (bits >> k) & 1:
+            place = place + (1 << k) * (1 - 2 * ((place // (1 << k)) % 2))
+    return place
+
+
 def joint_kernel(
     n, replicas,
-    residual, gate, up, weight, grads, index, value, right_ref, left_ref,
+    residual, gate, up, weight, grads, index, value, right, left,
     output, gate_grad, up_grad, weight_grad, update, updated, late,
     dall, slot_up, slot_dn, part, w_v, hidden, hidden_t,
-    index_v, value_v, word_v, amount_v, mixed, fin,
+    index_v, value_v, word_v, amount_v, mixed, fin, right_ref, left_ref,
     load_sem, comp_send, comp_recv, step_send, step_recv, chip_send, chip_recv,
     part_send, part_recv, late_sem,
 ):
@@ -181,9 +189,11 @@
         pltpu.make_async_copy(index, index_v.at[rep], load_sem.at[4]),
         pltpu.make_async_copy(value, value_v.at[rep], load_sem.at[5]),
         pltpu.make_async_copy(residual, output, load_sem.at[6]),
+        pltpu.make_async_copy(right, right_ref, load_sem.at[7]),
+        pltpu.make_async_copy(left, left_ref, load_sem.at[8]),
     ]
-    for load in loads:
-        load.start()
+    for i in (3, 0, 1):
+        loads[i].start()
 
     barrier = pltpu.get_barrier_semaphore()
     has_up, has_dn = z < chips - 1, z > 0
@@ -197,11 +207,10 @@
         pl.semaphore_signal(barrier, inc=1, device_id={"tp": me - 2}, device_id_type=MESH)
 
     pl.semaphore_signal(barrier, inc=1, device_id={"tp": partner}, device_id_type=MESH)
-    for step in range(1, replicas):
-        pl.semaphore_signal(
-            barrier, inc=1, device_id={"rep": (rep + step) % replicas}, device_id_type=MESH
-        )
-    pl.semaphore_wait(barrier, replicas + has_up.astype(jnp.int32) + has_dn.astype(jnp.int32))
+    rounds = replicas.bit_length() - 1
+    for turn in range(rounds):
+        pl.semaphore_signal(barrier, inc=1, device_id={"rep": flip(rep, 1 << turn)}, device_id_type=MESH)
+    pl.semaphore_wait(barrier, 1 + rounds + has_up.astype(jnp.int32) + has_dn.astype(jnp.int32))
 
     def send(way, s, src, dst):
         return pltpu.make_async_remote_copy(
@@ -229,15 +238,19 @@
             device_id={"tp": partner}, device_id_type=MESH,
         )
 
-    def comp_copies(step):
-        to = {"rep": (rep + step) % replicas}
-        return [
-            pltpu.make_async_remote_copy(
-                src_ref=src, dst_ref=dst.at[rep], send_sem=comp_send.at[kind, step - 1],
-                recv_sem=comp_recv.at[kind, step - 1], device_id=to, device_id_type=MESH,
-            )
-            for kind, (src, dst) in enumerate(((index, index_v), (value, value_v)))
-        ]
+    def comp_copies(turn):
+        copies = []
+        for m in range(1 << turn):
+            holder, spot = flip(rep, m), (1 << turn) - 1 + m
+            for kind, (own, all_v) in enumerate(((index, index_v), (value, value_v))):
+                copies.append(
+                    pltpu.make_async_remote_copy(
+                        src_ref=own if m == 0 else all_v.at[holder], dst_ref=all_v.at[holder],
+                        send_sem=comp_send.at[kind, spot], recv_sem=comp_recv.at[kind, spot],
+                        device_id={"rep": flip(rep, 1 << turn)}, device_id_type=MESH,
+                    )
+                )
+        return copies
 
     slots = (slot_up, slot_dn)
     rank = (z, chips - 1 - z)
@@ -250,9 +263,10 @@
             def _():
                 send(way, q, grads.at[pl.ds(q * piece, piece)], grad_piece(z, q)).start()
 
-    for step in range(1, replicas):
-        for copy in comp_copies(step):
-            copy.start()
+    for i in (2, 4, 5, 6, 7, 8):
+        loads[i].start()
+    for copy in comp_copies(0):
+        copy.start()
 
     loads[3].wait()
     for q in range(CHUNKS):
@@ -371,6 +385,14 @@
         lax.fori_loop(0, model // tile, make_part, 0)
         hand_over(target).start()
 
+        for turn in range(1, rounds):
+            @pl.when(k == turn - 1)
+            def _():
+                for copy in comp_copies(turn - 1):
+                    copy.wait_recv()
+                for copy in comp_copies(turn):
+                    copy.start()
+
         @pl.when(k > 0)
         def _():
             add_other(k - 1)
@@ -384,11 +406,10 @@
     loads[2].wait()
     lax.fori_loop(0, chips, make_target, 0)
 
-    for step in range(1, replicas):
-        for copy in comp_copies(step):
-            copy.wait_recv()
-    loads[4].wait()
-    loads[5].wait()
+    for copy in comp_copies(rounds - 1):
+        copy.wait_recv()
+    for i in (4, 5, 7, 8):
+        loads[i].wait()
 
     pairs = replicas // 2
     half = LANES // 2
@@ -530,8 +551,8 @@
     for chip in range(chips):
         for q in range(CHUNKS):
             to_partner(chip, q).wait_send()
-    for step in range(1, replicas):
-        for copy in comp_copies(step):
+    for turn in range(rounds):
+        for copy in comp_copies(turn):
             copy.wait_send()
     for way in range(2):
         @pl.when(onward[way])
@@ -568,11 +589,13 @@
         ((span_rows, replicas, listed), f32),
         ((listed // LANES * SPAN, LANES // TOPK * SPAN), bf16),
         ((block // CHUNKS, model), f32),
+        ((LANES // TOPK * SPAN, LANES // TOPK * SPAN), bf16),
+        ((SPAN, SPAN), bf16),
     ]
     total = sum(int(np.prod(shape)) * jnp.dtype(kind).itemsize for shape, kind in arrays)
     steps = chips * CHUNKS
     sems = [
-        dma((7,)), dma((2, replicas - 1)), dma((2, replicas - 1)), dma((2, steps)), dma((2, steps)),
+        dma((9,)), dma((2, replicas - 1)), dma((2, replicas - 1)), dma((2, steps)), dma((2, steps)),
         dma((steps,)), dma((steps,)), dma((chips,)), dma((chips,)), dma((CHUNKS,)),
     ]
     return total, [pltpu.VMEM(shape, kind) for shape, kind in arrays] + sems
@@ -589,7 +612,7 @@
         functools.partial(joint_kernel, n, replicas),
         out_shape=[pltpu.VMEM(shape, jnp.bfloat16) for shape in shapes]
         + [jax.ShapeDtypeStruct(residual_r.shape, jnp.bfloat16)],
-        in_specs=[any_spec] * 7 + [vmem_spec] * 2,
+        in_specs=[any_spec] * 9,
         out_specs=[vmem_spec] * 6 + [any_spec],
         scratch_shapes=scratch,
         compiler_params=pltpu.CompilerParams(
@@ -608,7 +631,7 @@
         out_shape=[jax.ShapeDtypeStruct(shape, jnp.bfloat16) for shape in shapes[1:]],
         in_specs=[vmem_spec] * 5,
         out_specs=[any_spec] * 5,
-        scratch_shapes=[pltpu.SemaphoreType.DMA((5,))],
+        scratch_shapes=[pltpu.SemaphoreType.DMA((5 * PUT_PARTS,))],
         compiler_params=pltpu.CompilerParams(vmem_limit_bytes=PUT_BYTES),
         cost_estimate=pl.CostEstimate(
             flops=2 * tokens * units * model, bytes_accessed=units * model * 8, transcendentals=0
@@ -622,7 +645,14 @@
 def put_kernel(*refs):
     sem = refs[-1]
     count = len(refs) // 2
-    copies = [pltpu.make_async_copy(refs[i], refs[count + i], sem.at[i]) for i in range(count)]
+    copies = []
+    for i in range(count):
+        rows = refs[i].shape[0] // PUT_PARTS
+        for k in range(PUT_PARTS):
+            at = pl.ds(k * rows, rows)
+            copies.append(
+                pltpu.make_async_copy(refs[i].at[at], refs[count + i].at[at], sem.at[i * PUT_PARTS + k])
+            )
     for copy in copies:
         copy.start()
     for copy in copies:
@@ -640,7 +670,7 @@
     span_rows, listed = comp_index.shape[1:]
     model = down_weight.shape[1]
     fits = False
-    if n % 4 == 0 and units % LANES == 0 and span_rows % 2 == 0 and replicas % 2 == 0:
+    if n % 4 == 0 and units % LANES == 0 and span_rows % 2 == 0 and replicas in (2, 4, 8):
         total, scratch = joint_scratch(n, replicas, tokens, units, model, span_rows, listed)
         fits = total < 36 * 2**20 and units >= chips_rows(n, tokens) and n // 2 == CHUNKS and 2 * CHUNKS >= CHUNKS - FIRST + span_rows // 3 + 2
     if fits:

time: 105 us -> 103 us (0.981)
  Pallas kernels: 96 us -> 94.1 us
    pallas_call x1, Pallas kernels: 87.1 us -> 85.3 us  [joint(): pl.pallas_call(functools.partial(joint_kernel, n, replicas), out_shape=[p...]
where the time goes in v4:
time: 103 us
  Pallas kernels  94.1 us (91%)
  waiting for transfers between devices  3.81 us (4%)
  starting transfers between devices  3.55 us (3%)
  other arithmetic  1.22 us (1%)
    pallas_call x1, Pallas kernels, joint(): pl.pallas_call(functools.partial(joint_kernel, n, replicas), out_shape=[p...  85.3 us
    pallas_call x1, Pallas kernels, joint(): pl.pallas_call(put_kernel, out_shape=[jax.ShapeDtypeStruct(shape, jnp.bfl...  8.74 us
    ppermute x1, waiting for transfers between devices, joint(): arrived = lax.ppermute(late, 'tp', hops)  3.81 us
    ppermute x1, starting transfers between devices, joint(): arrived = lax.ppermute(late, 'tp', hops)  3.55 us
  transfers between devices with their start and end apart: 1, of which 1 were waited for; matrix products, arithmetic and copies ran while one was open for 0% of the time, Pallas kernels for 8%

profile of v4, /device:TPU:0, one launch (start us, length us, event | category | flops | bytes accessed | tf_op | source)
XLA Modules:
  0.0 103.3 jit_solution(6159296034576780383)
XLA Ops:
  0.6 85.3 %joint.1 = (bf16[128,4096]{1,0:T(8,128)(2,1)S(1)}, bf16[1024,896]{1,0:T(8,128)(2,1)S(1)}, bf16[1024,896]{1,0:T(8,128)(2,1)S(1)}, bf16[896,4096]{1,0:T(8,128)(2,1...) custom-call(bf16[128,4096]{1,0:T(8,128)(2,1)} %bitcast.13, ...), custom_call_target="tpu_custom_call" | custom-call | flops 22548578304 | bytes 29360128 | tf_op jit(solution)/shard_map/joint/pallas_call | solution.py:611
  86.0 3.5 %collective-permute-start = (bf16[128,4096]{1,0:T(8,128)(2,1)}, bf16[128,4096]{1,0:T(8,128)(2,1)S(1)}, u32[]{:S(2)}, u32[]{:S(2)}) collective-permute-start(bf16[128,4096]{1,0:T(8,128)(2,1)} %get-tuple-element.19), channel_id=1, source_target_pairs={{0,2},{2,4},{4,6},{3,1},{5,3},{7,5},{8,10},{10,12},{12,14},{11,9},... | collective-permute-start | bytes 3145736 | tf_op jit(solution)/shard_map/ppermute | solution.py:627
  89.5 8.7 %put.1 = (bf16[1024,896]{1,0:T(8,128)(2,1)}, bf16[1024,896]{1,0:T(8,128)(2,1)}, bf16[896,4096]{1,0:T(8,128)(2,1)}, bf16[896,4096]{1,0:T(8,128)(2,1)}, bf16[896,4096]{1,0:T(8,128)(2,1)}) custom-call(bf16[1024,896]{1,0:T(8,128)(2,1)S(1)} %get-tuple-element.20.refs_0_, bf16[1024,896]{1,0:T(8,128)(2,1)S(1)} %get-tuple-element.21.refs_1_, ...), custom_call_target="tpu_custom_call" | custom-call | flops 7516192768 | bytes 29360128 | tf_op jit(solution)/shard_map/put/pallas_call | solution.py:629
  98.3 3.8 %collective-permute-done = bf16[128,4096]{1,0:T(8,128)(2,1)S(1)} collective-permute-done((bf16[128,4096]{1,0:T(8,128)(2,1)}, bf16[128,4096]{1,0:T(8,128)(2,1)S(1)}, u32[]{:S(2)}, u32[]{:S(2)}) %collective-permute-start) | collective-permute-done | bytes 1048608 | tf_op jit(solution)/shard_map/ppermute | solution.py:627
  102.1 1.2 %fusion = bf16[1,128,4096]{2,1,0:T(8,128)(2,1)} fusion(bf16[128,4096]{1,0:T(8,128)(2,1)S(1)} %collective-permute-done, bf16[128,4096]{1,0:T(8,128)(2,1)S(1)} %get-tuple-element.18), kind=kLoop, calls=%fused_computation.1 | loop fusion | flops 2097152 | bytes 3145728 | tf_op jit(solution)/shard_map/broadcast_in_dim | solution.py:682
Async XLA Ops:
  86.0 16.1 %collective-permute-start = (bf16[128,4096]{1,0:T(8,128)(2,1)}, bf16[128,4096]{1,0:T(8,128)(2,1)S(1)}, u32[]{:S(2)}, u32[]{:S(2)}) collective-permute-start(bf16[128,4096]{1,0:T(8,128)(2,1)} %get-tuple-element.19), channel_id=1, source_target_pairs={{0,2},{2,4},{4,6},{3,1},{5,3},{7,5},{8,10},{10,12},{12,14},{11,9},... | collective-permute-start | bytes 3145736 | tf_op jit(solution)/shard_map/ppermute | solution.py:627

commit v5 on v4

--- a/solution.py
+++ b/solution.py
@@ -192,8 +192,7 @@
         pltpu.make_async_copy(right, right_ref, load_sem.at[7]),
         pltpu.make_async_copy(left, left_ref, load_sem.at[8]),
     ]
-    for i in (3, 0, 1):
-        loads[i].start()
+    loads[3].start()
 
     barrier = pltpu.get_barrier_semaphore()
     has_up, has_dn = z < chips - 1, z > 0
@@ -210,6 +209,9 @@
     rounds = replicas.bit_length() - 1
     for turn in range(rounds):
         pl.semaphore_signal(barrier, inc=1, device_id={"rep": flip(rep, 1 << turn)}, device_id_type=MESH)
+    loads[0].start()
+    loads[1].start()
+    loads[3].wait()
     pl.semaphore_wait(barrier, 1 + rounds + has_up.astype(jnp.int32) + has_dn.astype(jnp.int32))
 
     def send(way, s, src, dst):
@@ -261,14 +263,13 @@
         for way in range(2):
             @pl.when(onward[way])
             def _():
-                send(way, q, grads.at[pl.ds(q * piece, piece)], grad_piece(z, q)).start()
+                send(way, q, grad_piece(z, q), grad_piece(z, q)).start()
 
     for i in (2, 4, 5, 6, 7, 8):
         loads[i].start()
     for copy in comp_copies(0):
         copy.start()
 
-    loads[3].wait()
     for q in range(CHUNKS):
         to_partner(z, q).start()
 

time: 103 us -> 103 us (level)
  no operation moved by 1% of the time
where the time goes in v5:
time: 103 us
  Pallas kernels  93.8 us (91%)
  waiting for transfers between devices  3.81 us (4%)
  starting transfers between devices  3.55 us (3%)
  other arithmetic  1.22 us (1%)
    pallas_call x1, Pallas kernels, joint(): pl.pallas_call(functools.partial(joint_kernel, n, replicas), out_shape=[p...  85.1 us
    pallas_call x1, Pallas kernels, joint(): pl.pallas_call(put_kernel, out_shape=[jax.ShapeDtypeStruct(shape, jnp.bfl...  8.74 us
    ppermute x1, waiting for transfers between devices, joint(): arrived = lax.ppermute(late, 'tp', hops)  3.81 us
    ppermute x1, starting transfers between devices, joint(): arrived = lax.ppermute(late, 'tp', hops)  3.55 us
  transfers between devices with their start and end apart: 1, of which 1 were waited for; matrix products, arithmetic and copies ran while one was open for 0% of the time, Pallas kernels for 8%

profile of v5, /device:TPU:0, one launch (start us, length us, event | category | flops | bytes accessed | tf_op | source)
XLA Modules:
  0.0 103.1 jit_solution(13600337268185913510)
XLA Ops:
  0.6 85.1 %joint.1 = (bf16[128,4096]{1,0:T(8,128)(2,1)S(1)}, bf16[1024,896]{1,0:T(8,128)(2,1)S(1)}, bf16[1024,896]{1,0:T(8,128)(2,1)S(1)}, bf16[896,4096]{1,0:T(8,128)(2,1...) custom-call(bf16[128,4096]{1,0:T(8,128)(2,1)} %bitcast.13, ...), custom_call_target="tpu_custom_call" | custom-call | flops 22548578304 | bytes 29360128 | tf_op jit(solution)/shard_map/joint/pallas_call | solution.py:612
  85.7 3.5 %collective-permute-start = (bf16[128,4096]{1,0:T(8,128)(2,1)}, bf16[128,4096]{1,0:T(8,128)(2,1)S(1)}, u32[]{:S(2)}, u32[]{:S(2)}) collective-permute-start(bf16[128,4096]{1,0:T(8,128)(2,1)} %get-tuple-element.19), channel_id=1, source_target_pairs={{0,2},{2,4},{4,6},{3,1},{5,3},{7,5},{8,10},{10,12},{12,14},{11,9},... | collective-permute-start | bytes 3145736 | tf_op jit(solution)/shard_map/ppermute | solution.py:628
  89.3 8.7 %put.1 = (bf16[1024,896]{1,0:T(8,128)(2,1)}, bf16[1024,896]{1,0:T(8,128)(2,1)}, bf16[896,4096]{1,0:T(8,128)(2,1)}, bf16[896,4096]{1,0:T(8,128)(2,1)}, bf16[896,4096]{1,0:T(8,128)(2,1)}) custom-call(bf16[1024,896]{1,0:T(8,128)(2,1)S(1)} %get-tuple-element.20.refs_0_, bf16[1024,896]{1,0:T(8,128)(2,1)S(1)} %get-tuple-element.21.refs_1_, ...), custom_call_target="tpu_custom_call" | custom-call | flops 7516192768 | bytes 29360128 | tf_op jit(solution)/shard_map/put/pallas_call | solution.py:630
  98.0 3.8 %collective-permute-done = bf16[128,4096]{1,0:T(8,128)(2,1)S(1)} collective-permute-done((bf16[128,4096]{1,0:T(8,128)(2,1)}, bf16[128,4096]{1,0:T(8,128)(2,1)S(1)}, u32[]{:S(2)}, u32[]{:S(2)}) %collective-permute-start) | collective-permute-done | bytes 1048608 | tf_op jit(solution)/shard_map/ppermute | solution.py:628
  101.8 1.2 %fusion = bf16[1,128,4096]{2,1,0:T(8,128)(2,1)} fusion(bf16[128,4096]{1,0:T(8,128)(2,1)S(1)} %collective-permute-done, bf16[128,4096]{1,0:T(8,128)(2,1)S(1)} %get-tuple-element.18), kind=kLoop, calls=%fused_computation.1 | loop fusion | flops 2097152 | bytes 3145728 | tf_op jit(solution)/shard_map/broadcast_in_dim | solution.py:683
Async XLA Ops:
  85.7 16.1 %collective-permute-start = (bf16[128,4096]{1,0:T(8,128)(2,1)}, bf16[128,4096]{1,0:T(8,128)(2,1)S(1)}, u32[]{:S(2)}, u32[]{:S(2)}) collective-permute-start(bf16[128,4096]{1,0:T(8,128)(2,1)} %get-tuple-element.19), channel_id=1, source_target_pairs={{0,2},{2,4},{4,6},{3,1},{5,3},{7,5},{8,10},{10,12},{12,14},{11,9},... | collective-permute-start | bytes 3145736 | tf_op jit(solution)/shard_map/ppermute | solution.py:628
